TPU v7x, 512 devices: a whole 4x4x16 slice. The times are simulated.
512 devices in a mesh: fft: 64 (over y, z), grp: 8 (over x, core).
Axes of the slice: x: 4, y: 4, z: 16, core: 2. Of those that a mesh axis runs over, the one named last changes fastest.
Arguments:
- potential: float32 [4, 256, 256, 256], P(None, 'fft', 'grp'), may hold values from -6 to 6
- stick_mill: int32 [2, 1024], replicated, may hold values from -128 to 127, as said below
- positions: int32 [3, 1024], P(None, 'grp'), may hold values from 0 to 255
- aug_charge: bfloat16 [171, 1024, 256], P(None, 'fft'), may hold values from -0.01171875 to 0.01171875
Outputs:
- vg_sticks: float32 [4, 2, 1024, 256], P(None, None, 'fft')
- d_matrix: float32 [4, 171, 1024], P(None, None, 'grp')
Inputs may be any that keep to these rules, and one draw needn't show every extreme that they name: `stick_mill`: stick k is owned by fft index k // 16; no two sticks have the same (gx, gy), and every stick has gx^2 + gy^2 < 128^2.
All inputs are finite; a program needn't handle non-finite values.
Results may differ from a plain program's by a relative error of at most 0.0029.
Values sent between devices are 32-bit elements; how exact they have to be, the bound alone decides.
No kernel may reach another device: no remote copies, remote signals or barrier semaphores. Data moves between devices by JAX's collectives and lax.ppermute only.
A program may use at most 128 MiB of HBM per device.

v0:
```python
import math

import jax
import jax.numpy as jnp
from jax import lax
from jax.sharding import PartitionSpec as P

two_pi = 2.0 * math.pi


def from_everyone(array, axis):
    copies = jnp.broadcast_to(array, (lax.axis_size(axis), *array.shape))
    return lax.all_to_all(copies, axis, split_axis=0, concat_axis=0, tiled=True)


def taken_together(array, axis):
    return from_everyone(array, axis).sum(axis=0)


def packed_total(arrays, axis):
    ends = [0]
    for a in arrays:
        ends.append(ends[-1] + a.size)
    subtotal = taken_together(jnp.concatenate([a.ravel() for a in arrays]), axis)
    return tuple((subtotal[b:e].reshape(a.shape) for a, b, e in zip(arrays, ends, ends[1:])))


def cut_along(array, dim, devices):
    before, after = (array.shape[:dim], array.shape[dim + 1 :])
    return jnp.moveaxis(array.reshape(*before, devices, -1, *after), dim, 0)


def sum_at_owner(array, axis, dim):
    parts = cut_along(array, dim, lax.axis_size(axis))
    arrived = lax.all_to_all(parts, axis, split_axis=0, concat_axis=0, tiled=True)
    return arrived.sum(axis=0)


def filled_up(lines, devices):
    spare = -lines.shape[0] % devices
    if not spare:
        return lines
    return jnp.concatenate([lines, jnp.zeros((spare, *lines.shape[1:]), lines.dtype)])


def in_order(parts, dim):
    dims = list(parts.shape[1:])
    dims[dim] *= parts.shape[0]
    return jnp.moveaxis(parts, 0, dim).reshape(dims)


def gathered_copies(array, axis, dim):
    return in_order(from_everyone(array, axis), dim)


def sum_by_parts(array, axes):
    lines = array.reshape(-1)
    own = sum_at_owner(filled_up(lines, lax.axis_size(axes)), axes, 0)
    whole = gathered_copies(own, axes, 0)
    return whole[: len(lines)].reshape(array.shape)


def z_transform(planes, grid_size):
    grid_index = jnp.arange(grid_size, dtype=jnp.int32)
    angle_z = (
        two_pi
        / grid_size
        * jnp.mod((grid_index[:, None] - grid_size // 2) * grid_index[None, :], grid_size).astype(
            jnp.float32
        )
    )
    cos_z = jnp.cos(angle_z)
    sin_z = jnp.sin(angle_z)
    high = lax.Precision.HIGHEST
    real_in = planes[0]
    imag_in = planes[1]
    real_out = jnp.einsum("tz,szk->skt", cos_z, real_in, precision=high) + jnp.einsum(
        "tz,szk->skt", sin_z, imag_in, precision=high
    )
    imag_out = jnp.einsum("tz,szk->skt", cos_z, imag_in, precision=high) - jnp.einsum(
        "tz,szk->skt", sin_z, real_in, precision=high
    )
    return jnp.stack([real_out, imag_out], axis=1) * float(grid_size) ** (-1.5)


def body(potential, stick_mill, positions, aug_charge):
    spin_count, plane_count, row_count, grid_size = potential.shape
    stick_total = stick_mill.shape[1]
    fft_count = lax.axis_size("fft")
    stick_local = stick_total // fft_count
    high = lax.Precision.HIGHEST
    grid_index = jnp.arange(grid_size, dtype=jnp.int32)
    angle_x = (
        two_pi
        / grid_size
        * jnp.mod(grid_index[:, None] * grid_index[None, :], grid_size).astype(jnp.float32)
    )
    dft_table = jnp.concatenate([jnp.cos(angle_x), -jnp.sin(angle_x)], axis=1)
    row_terms = jnp.dot(potential.reshape(-1, grid_size), dft_table, precision=high)
    real_x = row_terms[:, :grid_size].reshape(spin_count, plane_count, row_count, grid_size)
    imag_x = row_terms[:, grid_size:].reshape(spin_count, plane_count, row_count, grid_size)
    col_index = jnp.mod(stick_mill[0], grid_size)
    picked_re = jnp.take(real_x, col_index, axis=3)
    picked_im = jnp.take(imag_x, col_index, axis=3)
    row_global = lax.axis_index("grp") * row_count + jnp.arange(row_count, dtype=jnp.int32)
    angle_y = (
        two_pi
        / grid_size
        * jnp.mod(row_global[:, None] * stick_mill[1][None, :], grid_size).astype(jnp.float32)
    )
    cos_y = jnp.cos(angle_y)
    sin_y = jnp.sin(angle_y)
    part_re = jnp.einsum("szyk,yk->szk", picked_re, cos_y, precision=high) + jnp.einsum(
        "szyk,yk->szk", picked_im, sin_y, precision=high
    )
    part_im = jnp.einsum("szyk,yk->szk", picked_im, cos_y, precision=high) - jnp.einsum(
        "szyk,yk->szk", picked_re, sin_y, precision=high
    )
    whole_re, whole_im = packed_total((part_re, part_im), "grp")
    stacked = jnp.stack([whole_re, whole_im])
    planes = lax.all_to_all(stacked, "fft", split_axis=3, concat_axis=2, tiled=True)
    vg_local = z_transform(planes, grid_size)
    start = lax.axis_index("fft") * stick_local
    mine = lax.dynamic_slice_in_dim(stick_mill, start, stick_local, 1)
    shifted = grid_index - grid_size // 2
    phase_k = jnp.mod(
        mine[0][:, None, None] * positions[0][None, None, :]
        + mine[1][:, None, None] * positions[1][None, None, :]
        + shifted[None, :, None] * positions[2][None, None, :],
        grid_size,
    )
    angle_all = two_pi / grid_size * phase_k.astype(jnp.float32)
    cosine = jnp.cos(angle_all)
    sine = jnp.sin(angle_all)
    atom_count = positions.shape[1]
    charge = aug_charge.reshape(aug_charge.shape[0], stick_local * grid_size)
    results = []
    for channel in range(spin_count):
        mixed_term = (
            vg_local[channel, 0][:, :, None] * cosine - vg_local[channel, 1][:, :, None] * sine
        )
        mixed_half = mixed_term.astype(jnp.bfloat16).reshape(stick_local * grid_size, atom_count)
        results.append(jnp.dot(charge, mixed_half, preferred_element_type=jnp.float32))
    summed = sum_by_parts(jnp.stack(results), "fft")
    return (vg_local, summed)


def solution(mesh):
    placed = (P(None, "fft", "grp", None), P(), P(None, "grp"), P(None, "fft", None))
    return jax.shard_map(
        body,
        mesh=mesh,
        in_specs=placed,
        out_specs=(P(None, None, "fft", None), P(None, None, "grp")),
        check_vma=False,
    )
```

profile of v0, /device:TPU:8, one launch (start us, length us, event | category | flops | bytes accessed | tf_op | source)
XLA Modules:
  0.0 278.5 jit_solution(2292678514424314388)
XLA Ops:
  0.6 1.0 sine_negate_fusion
  1.7 0.8 fusion.99
  2.5 2.1 convolution_bitcast_fusion
  4.6 1.1 fusion.97
  5.7 2.0 copy.75
  7.7 2.7 copy.76
  10.4 14.5 %gather_fusion = f32[1024,4,4,32]{3,2,1,0:T(4,128)} fusion(f32[4,4,32,256]{2,1,3,0:T(4,128)S(1)} %copy.75, s32[1024]{0:T(1024)S(1)} %broadcast_clamp_fusion), kind=kCustom, calls=%fused_computation.clone | custom fusion | bytes 4198400 | tf_op jit(solution)/shard_map/jit(_take)/gather | solution.py:103
  24.9 16.2 %gather_fusion.1 = f32[1024,4,4,32]{3,2,1,0:T(4,128)} fusion(f32[4,4,32,256]{2,1,3,0:T(4,128)} %copy.76, s32[1024]{0:T(1024)S(1)} %broadcast_clamp_fusion), kind=kCustom, calls=%fused_computation.1.clone | custom fusion | bytes 4198400 | tf_op jit(solution)/shard_map/jit(_take)/gather | solution.py:104
  41.1 0.6 sine_bitcast_fusion
  41.7 1.0 copy.125
  42.7 1.0 copy.126
  43.7 32.1 %fusion.2 = (f32[1024,4,4]{2,1,0:T(4,128)}, f32[1024,4,4]{2,1,0:T(4,128)S(1)}, f32[1024,4,4]{2,1,0:T(4,128)}, f32[1024,4,4]{2,1,0:T(4,128)}) fusion(f32[1024,4,4,32]{3,2,1,0:T(4,128)} %gather_fusion, f32[1024,32]{1,0:T(8,128)} %copy.125, pred[1024]{0:T(1024)(128)(4,1)S(1)} %compare_and_fusion, f32[1024,32]{1,0:T(8,128)} %copy.126, ...), kind=kLoop, calls=%fused_computation.8 | loop fusion | flops 5177344 | bytes 4719616
  75.8 2.5 copy.104
  78.3 2.5 copy.98
  80.8 0.9 add_bitcast_fusion
  81.7 0.6 copy.127
  82.3 2.5 copy.110
  84.8 1.4 copy.116
  86.3 0.9 subtract_bitcast_fusion
  87.2 0.8 pad_maximum_fusion.1
  88.0 1.5 broadcast_in_dim.13
  89.6 4.9 %all-to-all-start = ((f32[8,1,32768]{2,1,0:T(1,128)}), f32[8,1,32768]{2,1,0:T(1,128)S(1)}, u32[]{:S(2)}, u32[]{:S(2)}) async-start(f32[8,1,32768]{2,1,0:T(1,128)} %broadcast_in_dim.13), calls=%async_computation | async-start | bytes 2097152 | tf_op jit(solution)/shard_map/all_to_all | solution.py:13
  94.4 0.8 constant_dynamic-slice_fusion
  95.2 15.1 %all-to-all-done = f32[8,1,32768]{2,1,0:T(1,128)S(1)} async-done(((f32[8,1,32768]{2,1,0:T(1,128)}), f32[8,1,32768]{2,1,0:T(1,128)S(1)}, u32[]{:S(2)}, u32[]{:S(2)}) %all-to-all-start) | async-done | bytes 1048608 | tf_op jit(solution)/shard_map/all_to_all | solution.py:13
  110.3 0.8 reduce_sum.18
  111.2 3.2 %copy.78 = f32[2,4,4,1024]{2,1,0,3:T(4,128)} copy(f32[2,4,4,1024]{3,2,1,0:T(4,128)S(1)} %pad_maximum_fusion.2) | data formatting | bytes 262144 | tf_op jit(solution)/shard_map/stack | solution.py:120
  114.4 6.6 %reshape.227 = f32[64,1,512]{2,1,0:T(1,128)} reshape(f32[1024,2,4,4]{3,2,1,0:T(4,128)} %bitcast.119) | data formatting | bytes 262144
  121.0 18.7 %all-to-all-start.1 = ((f32[64,1,512]{2,1,0:T(1,128)}), f32[64,1,512]{2,1,0:T(1,128)S(1)}, u32[]{:S(2)}, u32[]{:S(2)}) async-start(f32[64,1,512]{2,1,0:T(1,128)} %reshape.227), calls=%async_computation.1 | async-start | bytes 262144 | tf_op jit(solution)/shard_map/all_to_all | solution.py:121
  139.9 15.0 %all-to-all-done.1 = f32[64,1,512]{2,1,0:T(1,128)S(1)} async-done(((f32[64,1,512]{2,1,0:T(1,128)}), f32[64,1,512]{2,1,0:T(1,128)S(1)}, u32[]{:S(2)}, u32[]{:S(2)}) %all-to-all-start.1) | async-done | bytes 131104 | tf_op jit(solution)/shard_map/all_to_all | solution.py:121
  155.4 1.0 reduce.11
  156.4 6.8 %reshape.228 = f32[1024,2,4,4]{3,2,1,0:T(4,128)} reshape(f32[64,512]{1,0:T(8,128)S(1)} %reduce.11) | data formatting | bytes 262144
  163.1 5.6 %copy.121 = f32[2,4,4,64,16]{4,3,2,1,0:T(8,128)S(1)} copy(f32[2,4,4,64,16]{2,1,0,4,3:T(4,128)} %bitcast.118) | data formatting | bytes 262144 | tf_op jit(solution)/shard_map/all_to_all | solution.py:121
  169.2 1.8 fusion.44
  171.3 1.8 fusion.42
  173.2 1.8 fusion.8
  175.0 1.8 fusion.7
  176.9 9.1 %convolution_bitcast_fusion.4 = f32[1,171,128]{2,1,0:T(8,128)S(1)} fusion(f32[16,256]{1,0:T(8,128)S(1)} %get-tuple-element.32, s32[256,128]{1,0:T(8,128)S(1)} %broadcast_multiply_fusion, s32[16,128]{1,0:T(8,128)S(1)} %multiply_add_fusion, f32[16,256]{1,0:T(8,128)S(1)} %get-tuple-element.25, bf16[171,16,256]{2,1,0:T(8,128)(2,1)S(1)} %copy-done), kind=kOutput, calls=%fused_computation.26 | convolution fusion | flops 188743680 | bytes 1660416 | tf_op jit(solution)/shard_map/dot_general | solution.py:143
  186.0 9.3 %convolution_bitcast_fusion.3 = f32[1,171,128]{2,1,0:T(8,128)S(1)} fusion(f32[16,256]{1,0:T(8,128)S(1)} %get-tuple-element.30, f32[16,256]{1,0:T(8,128)S(1)} %get-tuple-element.31, s32[256,128]{1,0:T(8,128)S(1)} %broadcast_multiply_fusion, s32[16,128]{1,0:T(8,128)S(1)} %multiply_add_fusion, bf16[171,16,256]{2,1,0:T(8,128)(2,1)S(1)} %copy-done), kind=kOutput, calls=%fused_computation.25 | convolution fusion | flops 188743680 | bytes 1660416 | tf_op jit(solution)/shard_map/dot_general | solution.py:143
  195.3 8.8 %convolution_bitcast_fusion.2 = f32[1,171,128]{2,1,0:T(8,128)S(1)} fusion(f32[16,256]{1,0:T(8,128)S(1)} %get-tuple-element.28, f32[16,256]{1,0:T(8,128)S(1)} %get-tuple-element.29, s32[256,128]{1,0:T(8,128)S(1)} %broadcast_multiply_fusion, s32[16,128]{1,0:T(8,128)S(1)} %multiply_add_fusion, bf16[171,16,256]{2,1,0:T(8,128)(2,1)S(1)} %copy-done), kind=kOutput, calls=%fused_computation.24 | convolution fusion | flops 188743680 | bytes 1660416 | tf_op jit(solution)/shard_map/dot_general | solution.py:143
  204.1 9.0 %convolution_bitcast_fusion.1 = f32[1,171,128]{2,1,0:T(8,128)S(1)} fusion(f32[16,256]{1,0:T(8,128)S(1)} %get-tuple-element.26, f32[16,256]{1,0:T(8,128)S(1)} %get-tuple-element.27, s32[256,128]{1,0:T(8,128)S(1)} %broadcast_multiply_fusion, s32[16,128]{1,0:T(8,128)S(1)} %multiply_add_fusion, bf16[171,16,256]{2,1,0:T(8,128)(2,1)S(1)} %copy-done), kind=kOutput, calls=%fused_computation.23 | convolution fusion | flops 188743680 | bytes 1660416 | tf_op jit(solution)/shard_map/dot_general | solution.py:143
  213.2 0.6 all_to_all.32
  213.8 30.6 %all_to_all.37 = f32[64,1,1368]{2,1,0:T(1,128)S(1)} all-to-all(f32[64,1,1368]{2,1,0:T(1,128)S(1)} %all_to_all.32), channel_id=1, replica_groups=mesh['fft'=64,'grp'=8] {'fft'}, dimensions={0} | all-to-all | bytes 700416 | tf_op jit(solution)/shard_map/all_to_all | solution.py:35
  244.6 0.9 broadcast_in_dim.22
  245.5 6.7 %all-to-all-start.3 = ((f32[64,1,1368]{2,1,0:T(1,128)}), f32[64,1,1368]{2,1,0:T(1,128)S(1)}, u32[]{:S(2)}, u32[]{:S(2)}) async-start(f32[64,1,1368]{2,1,0:T(1,128)} %broadcast_in_dim.22), calls=%async_computation.3 | async-start | bytes 720896 | tf_op jit(solution)/shard_map/all_to_all | solution.py:13
  252.3 0.7 copy.91
  252.9 23.4 %all-to-all-done.3 = f32[64,1,1368]{2,1,0:T(1,128)S(1)} async-done(((f32[64,1,1368]{2,1,0:T(1,128)}), f32[64,1,1368]{2,1,0:T(1,128)S(1)}, u32[]{:S(2)}, u32[]{:S(2)}) %all-to-all-start.3) | async-done | bytes 350240 | tf_op jit(solution)/shard_map/all_to_all | solution.py:13
  276.3 0.9 reduce.6
  277.4 0.9 copy.92
  (26 shorter events, 2.1 us)
Async XLA Ops:
  0.6 176.3 %copy-start = (bf16[171,16,256]{2,1,0:T(8,128)(2,1)S(1)}, bf16[171,16,256]{2,1,0:T(8,128)(2,1)}, u32[]{:S(2)}) copy-start(bf16[171,16,256]{2,1,0:T(8,128)(2,1)} %param.9) | copy-start | bytes 4202500
  86.3 8.9 %copy-start.1 = (s32[3,128]{1,0:T(4,128)S(1)}, s32[3,128]{1,0:T(4,128)}, u32[]{:S(2)}) copy-start(s32[3,128]{1,0:T(4,128)} %param.8) | copy-start | bytes 4612
  89.6 20.8 %all-to-all-start = ((f32[8,1,32768]{2,1,0:T(1,128)}), f32[8,1,32768]{2,1,0:T(1,128)S(1)}, u32[]{:S(2)}, u32[]{:S(2)}) async-start(f32[8,1,32768]{2,1,0:T(1,128)} %broadcast_in_dim.13), calls=%async_computation | async-start | bytes 2097152 | tf_op jit(solution)/shard_map/all_to_all | solution.py:13
  121.0 33.9 %all-to-all-start.1 = ((f32[64,1,512]{2,1,0:T(1,128)}), f32[64,1,512]{2,1,0:T(1,128)S(1)}, u32[]{:S(2)}, u32[]{:S(2)}) async-start(f32[64,1,512]{2,1,0:T(1,128)} %reshape.227), calls=%async_computation.1 | async-start | bytes 262144 | tf_op jit(solution)/shard_map/all_to_all | solution.py:121
  245.5 30.8 %all-to-all-start.3 = ((f32[64,1,1368]{2,1,0:T(1,128)}), f32[64,1,1368]{2,1,0:T(1,128)S(1)}, u32[]{:S(2)}, u32[]{:S(2)}) async-start(f32[64,1,1368]{2,1,0:T(1,128)} %broadcast_in_dim.22), calls=%async_computation.3 | async-start | bytes 720896 | tf_op jit(solution)/shard_map/all_to_all | solution.py:13
where the time goes:
time: 282 us; the launch traced here: 278 us
  local copies, waits for them, and re-layouts  77.8 us (28%)
  waiting for transfers between devices  53.5 us (19%)
  matrix products  45.6 us (16%)
  other arithmetic  39.6 us (14%)
  blocking collectives  30.6 us (11%)
  starting transfers between devices  30.3 us (11%)
    all_to_all x2, waiting for transfers between devices, from_everyone(): return lax.all_to_all(copies, axis, split_axis=0, concat_axis=0, tiled=True)  38.5 us
    dot_general x4, matrix products, body(): jnp.dot(charge, mixed_half, preferred_element_type=jnp.float32)  36.2 us
    unnamed x4, other arithmetic  34.5 us
    all_to_all x1, blocking collectives, sum_at_owner(): lax.all_to_all(parts, axis, split_axis=0, concat_axis=0, tiled=True)  30.6 us
    all_to_all x1, starting transfers between devices, body(): lax.all_to_all(stacked, 'fft', split_axis=3, concat_axis=2, tiled=True)  18.7 us
    unnamed x12, local copies, waits for them, and re-layouts  17.6 us
    gather x1, local copies, waits for them, and re-layouts, body(): picked_im = jnp.take(imag_x, col_index, axis=3)  16.2 us
    all_to_all x1, waiting for transfers between devices, body(): lax.all_to_all(stacked, 'fft', split_axis=3, concat_axis=2, tiled=True)  15 us
  transfers between devices with their start and end apart: 3, of which 3 were waited for; matrix products, arithmetic and copies ran while one was open for 1% of the time, Pallas kernels for 0%

commit v1 on v0

v1 whole, which is shorter than its diff:
```python
import functools
import math

import jax
import jax.numpy as jnp
import numpy as np
from jax import lax
from jax.experimental import pallas as pl
from jax.experimental.pallas import tpu as pltpu
from jax.sharding import Mesh
from jax.sharding import PartitionSpec as P

N = 256
ROWS = ("y", "x", "core")
GRP = ("x", "core")
FFT = ("y", "z")
F32 = jnp.float32
BF16 = jnp.bfloat16


def split_table(table):
    high = table.astype(np.float32).astype(jnp.bfloat16)
    low = (table - high.astype(np.float64)).astype(np.float32).astype(jnp.bfloat16)
    return high, low


def wave_table(left, right):
    angle = 2.0 * math.pi / N * np.mod(np.outer(left, right), N)
    return np.concatenate([np.cos(angle), np.sin(angle)], axis=1)


def split_value(x):
    high = x.astype(BF16)
    return high, (x - high.astype(F32)).astype(BF16)


def dot(a, b):
    return jnp.dot(a, b, preferred_element_type=F32)


def plane_kernel(grp_ref, pot_ref, mill_ref, hi_ref, lo_ref, out_ref, stack, turned):
    cols = jnp.bitwise_and(mill_ref[...], N - 1)
    grid = lax.broadcasted_iota(jnp.int32, (N, 1024), 0)
    pick_x = jnp.where(grid == cols[0:1, :], 1.0, 0.0).astype(BF16)
    pick_y = jnp.where(grid == cols[1:2, :], 1.0, 0.0).astype(BF16)
    start = pl.multiple_of(grp_ref[0] * 32, 32)
    near_hi = hi_ref[pl.ds(start, 32), :]
    near_lo = lo_ref[pl.ds(start, 32), :]
    cos_y = dot(near_hi[:, :N], pick_y) + dot(near_lo[:, :N], pick_y)
    sin_y = dot(near_hi[:, N:], pick_y) + dot(near_lo[:, N:], pick_y)
    hi = hi_ref[...]
    lo = lo_ref[...]
    for c in range(4):
        p_hi, p_lo = split_value(pot_ref[c * 128 : (c + 1) * 128, :])
        wave = dot(p_hi, hi) + dot(p_hi, lo) + dot(p_lo, hi)
        w_hi, w_lo = split_value(wave)
        even = dot(w_hi[:, :N], pick_x) + dot(w_lo[:, :N], pick_x)
        odd = dot(w_hi[:, N:], pick_x) + dot(w_lo[:, N:], pick_x)
        for z in range(4):
            e = even[z * 32 : (z + 1) * 32, :]
            o = odd[z * 32 : (z + 1) * 32, :]
            real = jnp.sum(e * cos_y - o * sin_y, axis=0, keepdims=True)
            imag = -jnp.sum(e * sin_y + o * cos_y, axis=0, keepdims=True)
            for z0 in range(2):
                for j in range(2):
                    row = z0 * 64 + z * 16 + j * 4 + c
                    stack[row : row + 1, :] = real
                    stack[row + 8 : row + 9, :] = imag
    for b in range(8):
        turned[b * 128 : (b + 1) * 128, :] = stack[:, b * 128 : (b + 1) * 128].T
    lane = lax.broadcasted_iota(jnp.int32, (8, 128), 1)
    upper = lane >= 64
    second = jnp.bitwise_and(lane, 4) != 0
    for y in range(4):
        for g in range(8):
            base = y * 256 + g * 2
            parts = [turned[pl.ds(base + z0 * 16 + j, 8, 32), :] for z0 in range(2) for j in range(2)]
            tile = jnp.where(upper, jnp.where(second, parts[3], parts[2]), jnp.where(second, parts[1], parts[0]))
            at = (y * 8 + g) * 8
            out_ref[at : at + 8, :] = tile


def plane_part(potential, stick_mill, grp, hi, lo):
    return pl.pallas_call(
        plane_kernel,
        out_shape=jax.ShapeDtypeStruct((256, 128), F32),
        in_specs=[pl.BlockSpec(memory_space=pltpu.SMEM)] + [pl.BlockSpec(memory_space=pltpu.VMEM)] * 4,
        out_specs=pl.BlockSpec(memory_space=pltpu.VMEM),
        scratch_shapes=[pltpu.VMEM((128, 1024), F32), pltpu.VMEM((1024, 128), F32)],
        name="plane_part",
    )(grp, potential, stick_mill, hi, lo)


def fold_kernel(in_ref, out_ref):
    lane = lax.broadcasted_iota(jnp.int32, (8, 128), 1)
    lower = lane < 64
    sums = []
    for y in range(4):
        total = in_ref[y * 64 : y * 64 + 8, :]
        for g in range(1, 8):
            total = total + in_ref[y * 64 + g * 8 : y * 64 + g * 8 + 8, :]
        sums.append(total)
    for yp in range(2):
        a, b = sums[2 * yp], sums[2 * yp + 1]
        out_ref[pl.ds(yp, 8, 4), :] = jnp.where(lower, a, pltpu.roll(b, 64, 1))
        out_ref[pl.ds(2 + yp, 8, 4), :] = jnp.where(lower, pltpu.roll(a, 64, 1), b)


def folded(arrived):
    return pl.pallas_call(
        fold_kernel,
        out_shape=jax.ShapeDtypeStruct((32, 128), F32),
        in_specs=[pl.BlockSpec(memory_space=pltpu.VMEM)],
        out_specs=pl.BlockSpec(memory_space=pltpu.VMEM),
        name="fold",
    )(arrived)


def line_kernel(in_ref, hi_ref, lo_ref, out_ref):
    x = in_ref[...]
    t = jnp.concatenate([x, x, x, x], axis=0).T
    lane = lax.broadcasted_iota(jnp.int32, (16, 128), 1)
    halves = []
    for y0 in range(2):
        tile = t[y0 * 64 : y0 * 64 + 16, :]
        for z in range(1, 4):
            at = y0 * 64 + z * 16
            tile = jnp.where(lane >= 32 * z, t[at : at + 16, :], tile)
        halves.append(tile)
    a = jnp.concatenate(halves, axis=1)
    a_hi, a_lo = split_value(a)
    hi = hi_ref[...]
    r = dot(a_hi, hi) + dot(a_hi, lo_ref[...]) + dot(a_lo, hi)
    real = r[0:8, :N] + r[8:16, N:]
    imag = r[8:16, :N] - r[0:8, N:]
    for g in range(8):
        out_ref[g, 0:8, :] = real
        out_ref[g, 8:16, :] = imag


def line_part(arrived, hi, lo):
    return pl.pallas_call(
        line_kernel,
        out_shape=jax.ShapeDtypeStruct((8, 16, N), F32),
        in_specs=[pl.BlockSpec(memory_space=pltpu.VMEM)] * 3,
        out_specs=pl.BlockSpec(memory_space=pltpu.VMEM),
        name="line_part",
    )(arrived, hi, lo)


def phase_kernel(pos_ref, mill_ref, hi_ref, lo_ref, wave_ref, cos_ref, sin_ref):
    zcol = pos_ref[:, 2:3]
    grid = lax.broadcasted_iota(jnp.int32, (128, N), 1)
    pick = jnp.where(grid == zcol, 1.0, 0.0).astype(BF16)
    sign = 1.0 - 2.0 * jnp.bitwise_and(zcol, 1).astype(F32)
    wave_ref[...] = (dot(pick, hi_ref[...]) + dot(pick, lo_ref[...])) * sign
    k = pos_ref[:, 0:1] * mill_ref[0:1, :] + pos_ref[:, 1:2] * mill_ref[1:2, :]
    angle = (2.0 * math.pi / N) * jnp.bitwise_and(k, N - 1).astype(F32)
    cos_ref[...] = jnp.cos(angle)
    sin_ref[...] = jnp.sin(angle)


def phases(pos_cols, mine, hi, lo):
    return pl.pallas_call(
        phase_kernel,
        out_shape=(
            jax.ShapeDtypeStruct((128, 2 * N), F32),
            jax.ShapeDtypeStruct((128, 16), F32),
            jax.ShapeDtypeStruct((128, 16), F32),
        ),
        in_specs=[pl.BlockSpec(memory_space=pltpu.VMEM)] * 4,
        out_specs=(pl.BlockSpec(memory_space=pltpu.VMEM),) * 3,
        name="phases",
    )(pos_cols, mine, hi, lo)


def charge_kernel(v_ref, q_ref, wave_ref, ca_ref, sa_ref, vg_ref, d_ref, mixed):
    for s in range(16):
        g, j = s // 2, s % 2
        ca = ca_ref[:, s : s + 1]
        sa = sa_ref[:, s : s + 1]
        cb = wave_ref[:, :N]
        sb = wave_ref[:, N:]
        cosine = ca * cb - sa * sb
        sine = sa * cb + ca * sb
        for c in range(4):
            row = g * 16 + j * 4 + c
            real = v_ref[row : row + 1, :]
            imag = v_ref[row + 8 : row + 9, :]
            vg_ref[c, 0, s : s + 1, :] = real
            vg_ref[c, 1, s : s + 1, :] = imag
            mixed[c * 128 : (c + 1) * 128, s * N : (s + 1) * N] = (real * cosine - imag * sine).astype(BF16)
    d = lax.dot_general(q_ref[...], mixed[...], (((1,), (1,)), ((), ())), preferred_element_type=F32)
    for c in range(4):
        d_ref[pl.ds(c, 171, 4), :] = d[:, c * 128 : (c + 1) * 128]
    d_ref[684:704, :] = jnp.zeros((20, 128), F32)


def charge_part(v, charge, wave, ca, sa):
    return pl.pallas_call(
        charge_kernel,
        out_shape=(jax.ShapeDtypeStruct((4, 2, 16, N), F32), jax.ShapeDtypeStruct((704, 128), F32)),
        in_specs=[pl.BlockSpec(memory_space=pltpu.VMEM)] * 5,
        out_specs=(pl.BlockSpec(memory_space=pltpu.VMEM),) * 2,
        scratch_shapes=[pltpu.VMEM((512, 4096), BF16)],
        name="charge_part",
    )(v, charge, wave, ca, sa)


def total_kernel(in_ref, out_ref, half):
    total = in_ref[0:88, :]
    for m in range(1, 8):
        total = total + in_ref[m * 88 : (m + 1) * 88, :]
    half[...] = total
    own = half[0:11, :]
    for m in range(1, 8):
        own = own + half[m * 11 : (m + 1) * 11, :]
    for m in range(8):
        half[m * 11 : (m + 1) * 11, :] = own
    full = half[...]
    for m in range(8):
        out_ref[m * 88 : (m + 1) * 88, :] = full


def totals(arrived):
    return pl.pallas_call(
        total_kernel,
        out_shape=jax.ShapeDtypeStruct((704, 128), F32),
        in_specs=[pl.BlockSpec(memory_space=pltpu.VMEM)],
        out_specs=pl.BlockSpec(memory_space=pltpu.VMEM),
        scratch_shapes=[pltpu.VMEM((88, 128), F32)],
        name="totals",
    )(arrived)


def exchange(parts, axes):
    return lax.all_to_all(parts, axes, split_axis=0, concat_axis=0, tiled=True)


def tables():
    index = np.arange(N)
    flat = split_table(wave_table(index, index))
    y0, z4, zs, yp = np.meshgrid(np.arange(2), np.arange(4), np.arange(16), np.arange(2), indexing="ij")
    plane = (((2 * yp + y0) * 16 + zs) * 4 + z4).reshape(-1)
    line = split_table(wave_table(plane, index - N // 2) * float(N) ** -1.5)
    return flat, line


def body(potential, stick_mill, positions, aug_charge):
    (hi, lo), (line_hi, line_lo) = tables()
    hi, lo, line_hi, line_lo = map(jnp.asarray, (hi, lo, line_hi, line_lo))
    grp = lax.axis_index(GRP)
    fft = lax.axis_index(FFT)
    mine = lax.dynamic_slice_in_dim(stick_mill, fft * 16, 16, 1)
    part = plane_part(potential.reshape(512, N), stick_mill, grp.reshape(1), hi, lo)
    arrived = exchange(part.reshape(32, 8, 128), ROWS)
    lines = folded(arrived.reshape(256, 128))
    arrived = exchange(lines.reshape(16, 1, 256), "z")
    copies = line_part(arrived.reshape(32, 128), line_hi, line_lo)
    v = exchange(copies, GRP).reshape(128, N)
    wave, ca, sa = phases(positions.T, mine, hi, lo)
    vg, part = charge_part(v, aug_charge.reshape(171, 16 * N), wave, ca, sa)
    arrived = exchange(part.reshape(64, 1, 1408), FFT)
    own = totals(arrived.reshape(704, 128))
    whole = exchange(own.reshape(64, 1, 1408), FFT)
    return vg, jnp.moveaxis(whole.reshape(176, 4, 128)[:171], 1, 0)


def solution(mesh):
    fine = Mesh(mesh.devices.reshape(4, 16, 4, 2), ("y", "z", "x", "core"))
    placed = (P(None, FFT, GRP, None), P(), P(None, GRP), P(None, FFT, None))
    return jax.shard_map(
        body,
        mesh=fine,
        in_specs=placed,
        out_specs=(P(None, None, FFT, None), P(None, None, GRP)),
        check_vma=False,
    )
```

time: 282 us -> 132 us (0.47)
  the two profiles are of different devices: /device:TPU:8 before, /device:TPU:2 now
where the time goes in v1:
time: 132 us
  blocking collectives  104 us (79%)
  Pallas kernels  16.9 us (13%)
  local copies, waits for them, and re-layouts  5.33 us (4%)
  starting transfers between devices  4.69 us (4%)
    all_to_all x4, blocking collectives, exchange(): return lax.all_to_all(parts, axes, split_axis=0, concat_axis=0, tiled=True)  104 us
    pallas_call x1, Pallas kernels, plane_part(): pl.pallas_call(plane_kernel, out_shape=jax.ShapeDtypeStruct((256, 128), F...  5.32 us
    all_to_all x1, starting transfers between devices, exchange(): return lax.all_to_all(parts, axes, split_axis=0, concat_axis=0, tiled=True)  4.69 us
    pallas_call x1, Pallas kernels, charge_part(): pl.pallas_call(charge_kernel, out_shape=(jax.ShapeDtypeStruct((4, 2, 16,...  4.01 us
    unnamed x9, local copies, waits for them, and re-layouts  3.25 us
  transfers between devices with their start and end apart: 1, of which 0 were waited for; matrix products, arithmetic and copies ran while one was open for 3% of the time, Pallas kernels for 2%

profile of v1, /device:TPU:2, one launch (start us, length us, event | category | flops | bytes accessed | tf_op | source)
XLA Modules:
  0.0 131.7 jit_solution(5946017069992741449)
XLA Ops:
  0.6 0.0 copy-start
  0.6 5.3 %plane_part.1 = f32[256,128]{1,0:T(8,128)} custom-call(s32[1]{0:T(128)} %bitcast.grp_ref, f32[512,256]{1,0:T(8,128)} %bitcast.23, s32[2,1024]{1,0:T(2,128)} %mill_ref.1, bf16[256,512]{1,0:T(8,128)(2,1)} %constant.33.clone.hi_ref, bf16[256,512]{1,0:T(8,128)(2,1)} %constant.34.clone.lo_ref), custom_call_target="tpu_custom_call" | custom-call | tf_op jit(solution)/shard_map/plane_part/pallas_call | solution.py:84
  6.0 16.8 %all_to_all.25 = f32[32,8,128]{2,1,0:T(8,128)} all-to-all(f32[32,8,128]{2,1,0:T(8,128)} %bitcast.22), channel_id=1, replica_groups=mesh['y'=4,'z'=16,'x'=4,'core'=2] {'y','x','core'}, dimensions={0} | all-to-all | bytes 262144 | tf_op jit(solution)/shard_map/all_to_all | solution.py:237
  22.8 1.6 %fold.1 = f32[32,128]{1,0:T(8,128)} custom-call(f32[256,128]{1,0:T(8,128)} %bitcast.24), custom_call_target="tpu_custom_call" | custom-call | tf_op jit(solution)/shard_map/fold/pallas_call | solution.py:110
  24.3 25.3 %all_to_all.26 = f32[16,1,256]{2,1,0:T(1,128)} all-to-all(f32[16,1,256]{2,1,0:T(1,128)} %bitcast.28), channel_id=1, replica_groups=mesh['y'=4,'z'=16,'x'=4,'core'=2] {'z'}, dimensions={0} | all-to-all | bytes 32768 | tf_op jit(solution)/shard_map/all_to_all | solution.py:237
  49.7 2.0 %line_part.1 = f32[8,16,256]{2,1,0:T(8,128)} custom-call(f32[32,128]{1,0:T(8,128)} %bitcast.29, bf16[256,512]{1,0:T(8,128)(2,1)} %constant.35.clone.hi_ref, bf16[256,512]{1,0:T(8,128)(2,1)} %constant.36.clone.lo_ref), custom_call_target="tpu_custom_call" | custom-call | tf_op jit(solution)/shard_map/line_part/pallas_call | solution.py:142
  51.7 4.7 %all-to-all-start.2 = ((f32[8,16,256]{2,1,0:T(8,128)}), f32[8,16,256]{2,1,0:T(8,128)S(1)}, u32[]{:S(2)}, u32[]{:S(2)}) async-start(f32[8,16,256]{2,1,0:T(8,128)} %line_part.1), calls=%async_computation.2 | async-start | bytes 262144 | tf_op jit(solution)/shard_map/all_to_all | solution.py:237
  56.4 0.0 copy-done
  56.4 0.1 pad
  56.5 0.0 copy-start.2
  56.5 1.8 %copy.15 = bf16[22,8,16,256]{3,1,2,0:T(8,128)(2,1)} copy(bf16[22,8,16,256]{3,2,1,0:T(8,128)(2,1)S(1)} %bitcast.18) | data formatting | bytes 2883584
  58.2 0.0 copy-done.2
  58.2 0.7 copy.12
  59.0 1.3 %constant_dynamic-slice_fusion.mill_ref = s32[2,16]{1,0:T(2,128)} fusion(s32[2,1024]{1,0:T(2,128)} %mill_ref.1, s32[]{:T(128)S(6)} %select_n.3), kind=kLoop, calls=%fused_computation.1 | loop fusion | bytes 260 | tf_op jit(solution)/shard_map/dynamic_slice | solution.py:254
  60.3 2.2 %phases.1 = (f32[128,512]{1,0:T(8,128)}, f32[128,16]{1,0:T(8,128)}, f32[128,16]{1,0:T(8,128)}) custom-call(s32[128,3]{1,0:T(8,128)} %bitcast.27, s32[2,16]{1,0:T(2,128)} %constant_dynamic-slice_fusion.mill_ref, bf16[256,512]{1,0:T(8,128)(2,1)} %constant.33.clone.hi_ref, bf16[256,512]{1,0:T(8,128)(2,1)} %constant.34.clone.lo_ref), custom_call_target="tpu_custom_call" | custom-call | tf_op jit(solution)/shard_map/phases/pallas_call | solution.py:164
  62.5 0.0 all-to-all-done.2
  62.5 0.0 copy-start.1
  62.5 0.7 copy-done.1
  63.2 4.0 %charge_part.1 = (f32[4,2,16,256]{3,2,1,0:T(8,128)}, f32[704,128]{1,0:T(8,128)}) custom-call(f32[128,256]{1,0:T(8,128)} %bitcast.25, bf16[171,4096]{1,0:T(8,128)(2,1)} %bitcast.17, f32[128,512]{1,0:T(8,128)} %get-tuple-element.7.wave_ref, f32[128,16]{1,0:T(8,128)} %get-tuple-element.8.ca_ref, f32[128,16]{1,0:T(8,128)} %get-tuple-element.9.sa_ref), custom_call_target="tpu_custom_call" | custom-call | tf_op jit(solution)/shard_map/charge_part/pallas_call | solution.py:200
  67.2 31.0 %all_to_all.27 = f32[64,1,1408]{2,1,0:T(1,128)} all-to-all(f32[64,1,1408]{2,1,0:T(1,128)} %bitcast.26), channel_id=1, replica_groups=mesh['y'=4,'z'=16,'x'=4,'core'=2] {'y','z'}, dimensions={0} | all-to-all | bytes 720896 | tf_op jit(solution)/shard_map/all_to_all | solution.py:237
  98.2 1.8 %totals.1 = f32[704,128]{1,0:T(8,128)} custom-call(f32[704,128]{1,0:T(8,128)} %bitcast.19), custom_call_target="tpu_custom_call" | custom-call | tf_op jit(solution)/shard_map/totals/pallas_call | solution.py:226
  100.0 31.0 %all_to_all.28 = f32[64,1,1408]{2,1,0:T(1,128)S(1)} all-to-all(f32[64,1,1408]{2,1,0:T(1,128)} %bitcast.20), channel_id=1, replica_groups=mesh['y'=4,'z'=16,'x'=4,'core'=2] {'y','z'}, dimensions={0} | all-to-all | bytes 720896 | tf_op jit(solution)/shard_map/all_to_all | solution.py:237
  130.9 0.8 slice_bitcast_fusion
Async XLA Ops:
  0.6 55.7 %copy-start = (bf16[171,16,256]{2,1,0:T(8,128)(2,1)S(1)}, bf16[171,16,256]{2,1,0:T(8,128)(2,1)}, u32[]{:S(2)}) copy-start(bf16[171,16,256]{2,1,0:T(8,128)(2,1)} %param.11) | copy-start | bytes 4202500
  51.7 10.8 %all-to-all-start.2 = ((f32[8,16,256]{2,1,0:T(8,128)}), f32[8,16,256]{2,1,0:T(8,128)S(1)}, u32[]{:S(2)}, u32[]{:S(2)}) async-start(f32[8,16,256]{2,1,0:T(8,128)} %line_part.1), calls=%async_computation.2 | async-start | bytes 262144 | tf_op jit(solution)/shard_map/all_to_all | solution.py:237
  56.5 1.8 %copy-start.2 = (s32[3,128]{1,0:T(4,128)S(1)}, s32[3,128]{1,0:T(4,128)}, u32[]{:S(2)}) copy-start(s32[3,128]{1,0:T(4,128)} %param.10) | copy-start | bytes 4612
  62.5 0.7 copy-start.1

commit v2 on v1

--- a/solution.py
+++ b/solution.py
@@ -83,7 +83,7 @@
 def plane_part(potential, stick_mill, grp, hi, lo):
     return pl.pallas_call(
         plane_kernel,
-        out_shape=jax.ShapeDtypeStruct((256, 128), F32),
+        out_shape=pltpu.VMEM((256, 128), F32),
         in_specs=[pl.BlockSpec(memory_space=pltpu.SMEM)] + [pl.BlockSpec(memory_space=pltpu.VMEM)] * 4,
         out_specs=pl.BlockSpec(memory_space=pltpu.VMEM),
         scratch_shapes=[pltpu.VMEM((128, 1024), F32), pltpu.VMEM((1024, 128), F32)],
@@ -109,11 +109,11 @@
 def folded(arrived):
     return pl.pallas_call(
         fold_kernel,
-        out_shape=jax.ShapeDtypeStruct((32, 128), F32),
+        out_shape=pltpu.VMEM((32, 128), F32),
         in_specs=[pl.BlockSpec(memory_space=pltpu.VMEM)],
         out_specs=pl.BlockSpec(memory_space=pltpu.VMEM),
         name="fold",
-    )(arrived)
+    )(near(arrived))
 
 
 def line_kernel(in_ref, hi_ref, lo_ref, out_ref):
@@ -141,11 +141,11 @@
 def line_part(arrived, hi, lo):
     return pl.pallas_call(
         line_kernel,
-        out_shape=jax.ShapeDtypeStruct((8, 16, N), F32),
+        out_shape=pltpu.VMEM((8, 16, N), F32),
         in_specs=[pl.BlockSpec(memory_space=pltpu.VMEM)] * 3,
         out_specs=pl.BlockSpec(memory_space=pltpu.VMEM),
         name="line_part",
-    )(arrived, hi, lo)
+    )(near(arrived), hi, lo)
 
 
 def phase_kernel(pos_ref, mill_ref, hi_ref, lo_ref, wave_ref, cos_ref, sin_ref):
@@ -164,9 +164,9 @@
     return pl.pallas_call(
         phase_kernel,
         out_shape=(
-            jax.ShapeDtypeStruct((128, 2 * N), F32),
-            jax.ShapeDtypeStruct((128, 16), F32),
-            jax.ShapeDtypeStruct((128, 16), F32),
+            pltpu.VMEM((128, 2 * N), F32),
+            pltpu.VMEM((128, 16), F32),
+            pltpu.VMEM((128, 16), F32),
         ),
         in_specs=[pl.BlockSpec(memory_space=pltpu.VMEM)] * 4,
         out_specs=(pl.BlockSpec(memory_space=pltpu.VMEM),) * 3,
@@ -199,38 +199,66 @@
 def charge_part(v, charge, wave, ca, sa):
     return pl.pallas_call(
         charge_kernel,
-        out_shape=(jax.ShapeDtypeStruct((4, 2, 16, N), F32), jax.ShapeDtypeStruct((704, 128), F32)),
+        out_shape=(jax.ShapeDtypeStruct((4, 2, 16, N), F32), pltpu.VMEM((704, 128), F32)),
         in_specs=[pl.BlockSpec(memory_space=pltpu.VMEM)] * 5,
         out_specs=(pl.BlockSpec(memory_space=pltpu.VMEM),) * 2,
         scratch_shapes=[pltpu.VMEM((512, 4096), BF16)],
         name="charge_part",
-    )(v, charge, wave, ca, sa)
+    )(near(v), near(charge), near(wave), near(ca), near(sa))
+
+
+def meet_kernel(in_ref, out_ref):
+    out_ref[...] = (in_ref[0:176, :] + in_ref[176:352, :]) + (in_ref[352:528, :] + in_ref[528:704, :])
+
+
+def met(arrived):
+    return pl.pallas_call(
+        meet_kernel,
+        out_shape=pltpu.VMEM((176, 128), F32),
+        in_specs=[pl.BlockSpec(memory_space=pltpu.VMEM)],
+        out_specs=pl.BlockSpec(memory_space=pltpu.VMEM),
+        name="meet",
+    )(near(arrived))
 
 
 def total_kernel(in_ref, out_ref, half):
-    total = in_ref[0:88, :]
-    for m in range(1, 8):
-        total = total + in_ref[m * 88 : (m + 1) * 88, :]
-    half[...] = total
+    half[...] = in_ref[0:88, :] + in_ref[88:176, :]
     own = half[0:11, :]
     for m in range(1, 8):
         own = own + half[m * 11 : (m + 1) * 11, :]
-    for m in range(8):
-        half[m * 11 : (m + 1) * 11, :] = own
-    full = half[...]
-    for m in range(8):
-        out_ref[m * 88 : (m + 1) * 88, :] = full
+    for m in range(16):
+        out_ref[m * 11 : (m + 1) * 11, :] = own
 
 
 def totals(arrived):
     return pl.pallas_call(
         total_kernel,
-        out_shape=jax.ShapeDtypeStruct((704, 128), F32),
+        out_shape=pltpu.VMEM((176, 128), F32),
         in_specs=[pl.BlockSpec(memory_space=pltpu.VMEM)],
         out_specs=pl.BlockSpec(memory_space=pltpu.VMEM),
         scratch_shapes=[pltpu.VMEM((88, 128), F32)],
         name="totals",
-    )(arrived)
+    )(near(arrived))
+
+
+def copy_kernel(in_ref, out_ref):
+    x = in_ref[...]
+    for y in range(4):
+        out_ref[y * 176 : (y + 1) * 176, :] = x
+
+
+def four_copies(x):
+    return pl.pallas_call(
+        copy_kernel,
+        out_shape=pltpu.VMEM((704, 128), F32),
+        in_specs=[pl.BlockSpec(memory_space=pltpu.VMEM)],
+        out_specs=pl.BlockSpec(memory_space=pltpu.VMEM),
+        name="four_copies",
+    )(near(x))
+
+
+def near(x):
+    return pltpu.with_memory_space_constraint(x, pltpu.VMEM)
 
 
 def exchange(parts, axes):
@@ -256,13 +284,18 @@
     arrived = exchange(part.reshape(32, 8, 128), ROWS)
     lines = folded(arrived.reshape(256, 128))
     arrived = exchange(lines.reshape(16, 1, 256), "z")
+    wave, ca, sa = phases(positions.T, mine, hi, lo)
+    charge = aug_charge.reshape(171, 16 * N)
+    arrived, charge, wave, ca, sa = lax.optimization_barrier((arrived, charge, wave, ca, sa))
     copies = line_part(arrived.reshape(32, 128), line_hi, line_lo)
     v = exchange(copies, GRP).reshape(128, N)
-    wave, ca, sa = phases(positions.T, mine, hi, lo)
-    vg, part = charge_part(v, aug_charge.reshape(171, 16 * N), wave, ca, sa)
-    arrived = exchange(part.reshape(64, 1, 1408), FFT)
-    own = totals(arrived.reshape(704, 128))
-    whole = exchange(own.reshape(64, 1, 1408), FFT)
+    vg, part = charge_part(v, charge, wave, ca, sa)
+    arrived = exchange(part.reshape(4, 176, 128), "y")
+    mid = met(arrived.reshape(704, 128))
+    arrived = exchange(mid.reshape(16, 1, 1408), "z")
+    own = totals(arrived.reshape(176, 128))
+    line = exchange(own.reshape(16, 1, 1408), "z")
+    whole = exchange(four_copies(line.reshape(176, 128)).reshape(4, 176, 128), "y")
     return vg, jnp.moveaxis(whole.reshape(176, 4, 128)[:171], 1, 0)
 
 

time: 132 us -> 113 us (0.86)
  the two profiles are of different devices: /device:TPU:2 before, /device:TPU:32 now
where the time goes in v2:
time: 113 us
  blocking collectives  60.4 us (53%)
  starting transfers between devices  22.5 us (20%)
  waiting for transfers between devices  14.6 us (13%)
  Pallas kernels  11.1 us (10%)
  local copies, waits for them, and re-layouts  3.59 us (3%)
    all_to_all x5, blocking collectives, exchange(): return lax.all_to_all(parts, axes, split_axis=0, concat_axis=0, tiled=True)  60.4 us
    all_to_all x2, starting transfers between devices, exchange(): return lax.all_to_all(parts, axes, split_axis=0, concat_axis=0, tiled=True)  22.5 us
    all_to_all x2, waiting for transfers between devices, exchange(): return lax.all_to_all(parts, axes, split_axis=0, concat_axis=0, tiled=True)  14.6 us
    pallas_call x1, Pallas kernels, plane_part(): pl.pallas_call(plane_kernel, out_shape=pltpu.VMEM((256, 128), F32), in_sp...  5.33 us
  transfers between devices with their start and end apart: 2, of which 2 were waited for; matrix products, arithmetic and copies ran while one was open for 2% of the time, Pallas kernels for 1%

profile of v2, /device:TPU:32, one launch (start us, length us, event | category | flops | bytes accessed | tf_op | source)
XLA Modules:
  0.0 112.9 jit_solution(2161211709612133709)
XLA Ops:
  0.6 0.0 copy-start
  0.6 5.3 %plane_part.1 = f32[256,128]{1,0:T(8,128)} custom-call(s32[1]{0:T(128)} %bitcast.grp_ref, f32[512,256]{1,0:T(8,128)} %bitcast.34, s32[2,1024]{1,0:T(2,128)} %mill_ref.1, bf16[256,512]{1,0:T(8,128)(2,1)} %constant.33.clone.hi_ref, bf16[256,512]{1,0:T(8,128)(2,1)} %constant.34.clone.lo_ref), custom_call_target="tpu_custom_call" | custom-call | tf_op jit(solution)/shard_map/plane_part/pallas_call | solution.py:84
  6.0 7.3 %all-to-all-start = ((f32[32,8,128]{2,1,0:T(8,128)}), f32[32,8,128]{2,1,0:T(8,128)S(1)}, u32[]{:S(2)}, u32[]{:S(2)}) async-start(f32[32,8,128]{2,1,0:T(8,128)} %bitcast.2), calls=%async_computation | async-start | bytes 262144 | tf_op jit(solution)/shard_map/all_to_all | solution.py:265
  13.3 0.0 copy-done
  13.3 0.1 pad
  13.4 0.0 copy-start.1
  13.4 0.6 copy.15
  14.1 0.0 copy-done.1
  14.1 0.7 copy.12
  14.8 6.2 %all-to-all-done = f32[32,8,128]{2,1,0:T(8,128)S(1)} async-done(((f32[32,8,128]{2,1,0:T(8,128)}), f32[32,8,128]{2,1,0:T(8,128)S(1)}, u32[]{:S(2)}, u32[]{:S(2)}) %all-to-all-start) | async-done | bytes 131104 | tf_op jit(solution)/shard_map/all_to_all | solution.py:265
  21.1 0.7 fold.1
  21.8 15.2 %all-to-all-start.1 = ((f32[16,1,256]{2,1,0:T(1,128)}), f32[16,1,256]{2,1,0:T(1,128)S(1)}, u32[]{:S(2)}, u32[]{:S(2)}) async-start(f32[16,1,256]{2,1,0:T(1,128)} %bitcast.4), calls=%async_computation.1 | async-start | bytes 32768 | tf_op jit(solution)/shard_map/all_to_all | solution.py:265
  37.0 1.3 %constant_dynamic-slice_fusion.mill_ref = s32[2,16]{1,0:T(2,128)} fusion(s32[2,1024]{1,0:T(2,128)} %mill_ref.1, s32[]{:T(128)S(6)} %select_n.3), kind=kLoop, calls=%fused_computation.1 | loop fusion | bytes 260 | tf_op jit(solution)/shard_map/dynamic_slice | solution.py:282
  38.3 1.5 %phases.1 = (f32[128,512]{1,0:T(8,128)S(1)}, f32[128,16]{1,0:T(8,128)S(1)}, f32[128,16]{1,0:T(8,128)S(1)}) custom-call(s32[128,3]{1,0:T(8,128)} %bitcast.35, s32[2,16]{1,0:T(2,128)} %constant_dynamic-slice_fusion.mill_ref, bf16[256,512]{1,0:T(8,128)(2,1)} %constant.33.clone.hi_ref, bf16[256,512]{1,0:T(8,128)(2,1)} %constant.34.clone.lo_ref), custom_call_target="tpu_custom_call" | custom-call | tf_op jit(solution)/shard_map/phases/pallas_call | solution.py:164
  39.8 8.4 %all-to-all-done.1 = f32[16,1,256]{2,1,0:T(1,128)S(1)} async-done(((f32[16,1,256]{2,1,0:T(1,128)}), f32[16,1,256]{2,1,0:T(1,128)S(1)}, u32[]{:S(2)}, u32[]{:S(2)}) %all-to-all-start.1) | async-done | bytes 16416 | tf_op jit(solution)/shard_map/all_to_all | solution.py:265
  48.2 1.3 %line_part.1 = f32[8,16,256]{2,1,0:T(8,128)S(1)} custom-call(f32[32,128]{1,0:T(8,128)S(1)} %bitcast.31, bf16[256,512]{1,0:T(8,128)(2,1)} %constant.35.clone.hi_ref, bf16[256,512]{1,0:T(8,128)(2,1)} %constant.36.clone.lo_ref), custom_call_target="tpu_custom_call" | custom-call | tf_op jit(solution)/shard_map/line_part/pallas_call | solution.py:142
  49.5 8.5 %all_to_all.35 = f32[8,16,256]{2,1,0:T(8,128)S(1)} all-to-all(f32[8,16,256]{2,1,0:T(8,128)S(1)} %line_part.1), channel_id=1, replica_groups=mesh['y'=4,'z'=16,'x'=4,'core'=2] {'x','core'}, dimensions={0} | all-to-all | bytes 262144 | tf_op jit(solution)/shard_map/all_to_all | solution.py:265
  58.0 2.2 %charge_part.1 = (f32[4,2,16,256]{3,2,1,0:T(8,128)}, f32[704,128]{1,0:T(8,128)S(1)}) custom-call(f32[128,256]{1,0:T(8,128)S(1)} %bitcast.25, bf16[171,4096]{1,0:T(8,128)(2,1)S(1)} %bitcast.21, f32[128,512]{1,0:T(8,128)S(1)} %get-tuple-element.17.wave_ref, f32[128,16]{1,0:T(8,128)S(1)} %get-tuple-element.18.ca_ref, f32[128,16]{1,0:T(8,128)S(1)} %get-tuple-element.19.sa_ref), custom_call_target="tpu_custom_call" | custom-call | tf_op jit(solution)/shard_map/charge_part/pallas_call | solution.py:200
  60.2 10.2 %all_to_all.36 = f32[4,176,128]{2,1,0:T(8,128)S(1)} all-to-all(f32[4,176,128]{2,1,0:T(8,128)S(1)} %bitcast.28), channel_id=1, replica_groups=mesh['y'=4,'z'=16,'x'=4,'core'=2] {'y'}, dimensions={0} | all-to-all | bytes 720896 | tf_op jit(solution)/shard_map/all_to_all | solution.py:265
  70.4 16.0 %all_to_all.37 = f32[16,1,1408]{2,1,0:T(1,128)S(1)} all-to-all(f32[16,1,1408]{2,1,0:T(1,128)S(1)} %bitcast.26), channel_id=1, replica_groups=mesh['y'=4,'z'=16,'x'=4,'core'=2] {'z'}, dimensions={0} | all-to-all | bytes 180224 | tf_op jit(solution)/shard_map/all_to_all | solution.py:265
  86.5 16.1 %all_to_all.38 = f32[16,1,1408]{2,1,0:T(1,128)S(1)} all-to-all(f32[16,1,1408]{2,1,0:T(1,128)S(1)} %bitcast.30), channel_id=1, replica_groups=mesh['y'=4,'z'=16,'x'=4,'core'=2] {'z'}, dimensions={0} | all-to-all | bytes 180224 | tf_op jit(solution)/shard_map/all_to_all | solution.py:265
  102.6 9.6 %all_to_all.39 = f32[4,176,128]{2,1,0:T(8,128)S(1)} all-to-all(f32[4,176,128]{2,1,0:T(8,128)S(1)} %bitcast.23), channel_id=1, replica_groups=mesh['y'=4,'z'=16,'x'=4,'core'=2] {'y'}, dimensions={0} | all-to-all | bytes 720896 | tf_op jit(solution)/shard_map/all_to_all | solution.py:265
  112.2 0.8 slice_bitcast_fusion
  (3 shorter events, 0.1 us)
Async XLA Ops:
  0.6 12.7 %copy-start = (bf16[171,16,256]{2,1,0:T(8,128)(2,1)S(1)}, bf16[171,16,256]{2,1,0:T(8,128)(2,1)}, u32[]{:S(2)}) copy-start(bf16[171,16,256]{2,1,0:T(8,128)(2,1)} %param.11) | copy-start | bytes 4202500
  6.0 15.1 %all-to-all-start = ((f32[32,8,128]{2,1,0:T(8,128)}), f32[32,8,128]{2,1,0:T(8,128)S(1)}, u32[]{:S(2)}, u32[]{:S(2)}) async-start(f32[32,8,128]{2,1,0:T(8,128)} %bitcast.2), calls=%async_computation | async-start | bytes 262144 | tf_op jit(solution)/shard_map/all_to_all | solution.py:265
  13.4 0.7 copy-start.1
  21.8 26.4 %all-to-all-start.1 = ((f32[16,1,256]{2,1,0:T(1,128)}), f32[16,1,256]{2,1,0:T(1,128)S(1)}, u32[]{:S(2)}, u32[]{:S(2)}) async-start(f32[16,1,256]{2,1,0:T(1,128)} %bitcast.4), calls=%async_computation.1 | async-start | bytes 32768 | tf_op jit(solution)/shard_map/all_to_all | solution.py:265

commit v3 on v2

v3 whole, which is shorter than its diff:
```python
import math

import jax
import jax.numpy as jnp
import numpy as np
from jax import lax
from jax.experimental import pallas as pl
from jax.experimental.pallas import tpu as pltpu
from jax.sharding import Mesh
from jax.sharding import PartitionSpec as P

N = 256
H = 128
GRP = ("x", "core")
FFT = ("y", "zh", "zl")
F32 = jnp.float32
BF16 = jnp.bfloat16
VMEM = pl.BlockSpec(memory_space=pltpu.VMEM)


def split_table(table):
    high = table.astype(np.float32).astype(jnp.bfloat16)
    low = (table - high.astype(np.float64)).astype(np.float32).astype(jnp.bfloat16)
    return high, low


def wave_table(left, right):
    angle = 2.0 * math.pi / N * np.mod(np.outer(left, right), N)
    return np.concatenate([np.cos(angle), np.sin(angle)], axis=1)


def tables():
    index = np.arange(N)
    flat = split_table(wave_table(index, index[:H]))
    z4, f = np.meshgrid(np.arange(4), np.arange(64), indexing="ij")
    plane = (f * 4 + z4).reshape(-1)
    line = split_table(wave_table(plane, index - N // 2) * float(N) ** -1.5)
    return flat, line


def split_value(x):
    high = x.astype(BF16)
    return high, (x - high.astype(F32)).astype(BF16)


def dot(a, b):
    return jnp.dot(a, b, preferred_element_type=F32)


def near(x):
    return pltpu.with_memory_space_constraint(x, pltpu.VMEM)


def picks(index):
    grid = lax.broadcasted_iota(jnp.int32, (H, 1024), 0)
    hit = grid == jnp.abs(index)
    even = jnp.where(hit, 1.0, 0.0).astype(BF16)
    odd = jnp.where(hit, jnp.where(index < 0, -1.0, 1.0), 0.0).astype(BF16)
    return jnp.concatenate([even, even], axis=0), jnp.concatenate([odd, odd], axis=0)


def plane_kernel(grp_ref, pot_ref, mill_ref, hi_ref, lo_ref, out_ref, stack, turned):
    start = pl.multiple_of(grp_ref[0] * 32, 32)
    near_hi = hi_ref[pl.ds(start, 32), :]
    near_lo = lo_ref[pl.ds(start, 32), :]
    even_y, odd_y = picks(mill_ref[1:2, :])
    cos_y = dot(jnp.concatenate([near_hi[:, :H], near_lo[:, :H]], axis=1), even_y)
    sin_y = dot(jnp.concatenate([near_hi[:, H:], near_lo[:, H:]], axis=1), odd_y)
    even_x, odd_x = picks(mill_ref[0:1, :])
    hi = hi_ref[...]
    wide = jnp.concatenate([hi, lo_ref[...], hi], axis=0)
    for c in range(4):
        p_hi, p_lo = split_value(pot_ref[c * 128 : (c + 1) * 128, :])
        wave = dot(jnp.concatenate([p_hi, p_hi, p_lo], axis=1), wide)
        w_hi, w_lo = split_value(wave)
        even = dot(jnp.concatenate([w_hi[:, :H], w_lo[:, :H]], axis=1), even_x)
        odd = dot(jnp.concatenate([w_hi[:, H:], w_lo[:, H:]], axis=1), odd_x)
        for z in range(4):
            e = even[z * 32 : (z + 1) * 32, :]
            o = odd[z * 32 : (z + 1) * 32, :]
            real = jnp.sum(e * cos_y - o * sin_y, axis=0, keepdims=True)
            imag = -jnp.sum(e * sin_y + o * cos_y, axis=0, keepdims=True)
            for j in range(4):
                row = z * 32 + j * 4 + c
                stack[row : row + 1, :] = real
                stack[row + 16 : row + 17, :] = imag
    for b in range(8):
        turned[b * 128 : (b + 1) * 128, :] = stack[:, b * 128 : (b + 1) * 128].T
    lane = lax.broadcasted_iota(jnp.int32, (16, 128), 1)
    upper = jnp.bitwise_and(lane, 8) != 0
    second = jnp.bitwise_and(lane, 4) != 0
    for y in range(4):
        for x in range(4):
            base = y * 256 + x * 4
            parts = [turned[pl.ds(base + j, 16, 16), :] for j in range(4)]
            tile = jnp.where(upper, jnp.where(second, parts[3], parts[2]), jnp.where(second, parts[1], parts[0]))
            at = (y * 4 + x) * 16
            out_ref[at : at + 16, :] = tile


def plane_part(potential, stick_mill, grp, hi, lo):
    return pl.pallas_call(
        plane_kernel,
        out_shape=pltpu.VMEM((256, 128), F32),
        in_specs=[pl.BlockSpec(memory_space=pltpu.SMEM)] + [VMEM] * 4,
        out_specs=VMEM,
        scratch_shapes=[pltpu.VMEM((128, 1024), F32), pltpu.VMEM((1024, 128), F32)],
        name="plane_part",
    )(grp, potential, stick_mill, hi, lo)


def fold_kernel(in_ref, out_ref):
    for y in range(4):
        at = y * 64
        total = (in_ref[at : at + 16, :] + in_ref[at + 16 : at + 32, :]) + (
            in_ref[at + 32 : at + 48, :] + in_ref[at + 48 : at + 64, :]
        )
        for core in range(2):
            out_ref[pl.ds(core * 4 + y, 16, 8), :] = total


def folded(arrived):
    return pl.pallas_call(
        fold_kernel,
        out_shape=pltpu.VMEM((128, 128), F32),
        in_specs=[VMEM],
        out_specs=VMEM,
        name="fold",
    )(near(arrived))


def line_kernel(in_ref, hi_ref, lo_ref, out_ref):
    rows = [in_ref[pl.ds(y, 16, 8), :] + in_ref[pl.ds(y + 4, 16, 8), :] for y in range(4)]
    t = jnp.concatenate(rows + rows, axis=0).T
    lower = lax.broadcasted_iota(jnp.int32, (32, 128), 1) < 64
    halves = [jnp.where(lower, t[b * 64 : b * 64 + 32, :], t[b * 64 + 32 : b * 64 + 64, :]) for b in range(2)]
    a_hi, a_lo = split_value(jnp.concatenate(halves, axis=1))
    hi = hi_ref[...]
    r = dot(a_hi, hi) + dot(a_hi, lo_ref[...]) + dot(a_lo, hi)
    real = r[0:16, :N] + r[16:32, N:]
    imag = r[16:32, :N] - r[0:16, N:]
    for x in range(4):
        out_ref[x, 0:16, :] = real
        out_ref[x, 16:32, :] = imag


def line_part(arrived, hi, lo):
    return pl.pallas_call(
        line_kernel,
        out_shape=pltpu.VMEM((4, 32, N), F32),
        in_specs=[VMEM] * 3,
        out_specs=VMEM,
        name="line_part",
    )(near(arrived), near(hi), near(lo))


def phase_kernel(pos_ref, mill_ref, hi_ref, lo_ref, wave_ref, cos_ref, sin_ref):
    zcol = pos_ref[:, 2:3]
    grid = lax.broadcasted_iota(jnp.int32, (128, N), 1)
    pick = jnp.where(grid == zcol, 1.0, 0.0).astype(BF16)
    sign = 1.0 - 2.0 * jnp.bitwise_and(zcol, 1).astype(F32)
    wave = dot(pick, hi_ref[...]) + dot(pick, lo_ref[...])
    turn = wave * sign
    wave_ref[:, 0:H] = turn[:, :H]
    wave_ref[:, H:N] = wave[:, :H]
    wave_ref[:, N : N + H] = turn[:, H:]
    wave_ref[:, N + H :] = wave[:, H:]
    k = pos_ref[:, 0:1] * mill_ref[0:1, :] + pos_ref[:, 1:2] * mill_ref[1:2, :]
    angle = (2.0 * math.pi / N) * jnp.bitwise_and(k, N - 1).astype(F32)
    cos_ref[...] = jnp.cos(angle)
    sin_ref[...] = jnp.sin(angle)


def phases(pos_cols, mine, hi, lo):
    return pl.pallas_call(
        phase_kernel,
        out_shape=(
            pltpu.VMEM((128, 2 * N), F32),
            pltpu.VMEM((128, 16), F32),
            pltpu.VMEM((128, 16), F32),
        ),
        in_specs=[VMEM] * 4,
        out_specs=(VMEM,) * 3,
        name="phases",
    )(pos_cols, mine, hi, lo)


def charge_kernel(v_ref, far_ref, wave_ref, ca_ref, sa_ref, vg_ref, d_ref, mixed, q_ref, done):
    load = pltpu.make_async_copy(far_ref, q_ref, done)
    load.start()
    for s in range(16):
        ca = ca_ref[:, s : s + 1]
        sa = sa_ref[:, s : s + 1]
        cb = wave_ref[:, :N]
        sb = wave_ref[:, N:]
        cosine = ca * cb - sa * sb
        sine = sa * cb + ca * sb
        for c in range(4):
            row = (s // 4) * 32 + (s % 4) * 4 + c
            real = v_ref[row : row + 1, :]
            imag = v_ref[row + 16 : row + 17, :]
            vg_ref[c, 0, s : s + 1, :] = real
            vg_ref[c, 1, s : s + 1, :] = imag
            mixed[c * 128 : (c + 1) * 128, s * N : (s + 1) * N] = (real * cosine - imag * sine).astype(BF16)
    load.wait()
    d = lax.dot_general(q_ref[...], mixed[...], (((1,), (1,)), ((), ())), preferred_element_type=F32)
    for c in range(4):
        d_ref[pl.ds(c, 171, 4), :] = d[:, c * 128 : (c + 1) * 128]
    d_ref[684:704, :] = jnp.zeros((20, 128), F32)


def charge_part(v, charge, wave, ca, sa):
    return pl.pallas_call(
        charge_kernel,
        out_shape=(jax.ShapeDtypeStruct((4, 2, 16, N), F32), pltpu.VMEM((704, 128), F32)),
        in_specs=[VMEM, pl.BlockSpec(memory_space=pl.ANY), VMEM, VMEM, VMEM],
        out_specs=(VMEM,) * 2,
        scratch_shapes=[
            pltpu.VMEM((512, 4096), BF16),
            pltpu.VMEM((171, 4096), BF16),
            pltpu.SemaphoreType.DMA(()),
        ],
        name="charge_part",
    )(near(v), charge, near(wave), near(ca), near(sa))


def meet_kernel(in_ref, out_ref, half):
    total = in_ref[0:88, :]
    for m in range(1, 8):
        total = total + in_ref[m * 88 : (m + 1) * 88, :]
    half[...] = total
    own = half[0:44, :] + half[44:88, :]
    for m in range(4):
        out_ref[m * 44 : (m + 1) * 44, :] = own


def met(arrived):
    return pl.pallas_call(
        meet_kernel,
        out_shape=pltpu.VMEM((176, 128), F32),
        in_specs=[VMEM],
        out_specs=VMEM,
        scratch_shapes=[pltpu.VMEM((88, 128), F32)],
        name="meet",
    )(near(arrived))


def total_kernel(in_ref, out_ref, half):
    half[...] = in_ref[0:88, :] + in_ref[88:176, :]
    own = half[0:44, :] + half[44:88, :]
    half[0:44, :] = own
    half[44:88, :] = own
    pair = half[...]
    for m in range(8):
        out_ref[m * 88 : (m + 1) * 88, :] = pair


def totals(arrived):
    return pl.pallas_call(
        total_kernel,
        out_shape=pltpu.VMEM((704, 128), F32),
        in_specs=[VMEM],
        out_specs=VMEM,
        scratch_shapes=[pltpu.VMEM((88, 128), F32)],
        name="totals",
    )(near(arrived))


def exchange(parts, axes):
    return lax.all_to_all(parts, axes, split_axis=0, concat_axis=0, tiled=True)


def body(potential, stick_mill, positions, aug_charge):
    (hi, lo), (line_hi, line_lo) = tables()
    hi, lo, line_hi, line_lo = map(jnp.asarray, (hi, lo, line_hi, line_lo))
    grp = lax.axis_index(GRP)
    fft = lax.axis_index(FFT)
    mine = lax.dynamic_slice_in_dim(stick_mill, fft * 16, 16, 1)
    part = plane_part(potential.reshape(512, N), stick_mill, grp.reshape(1), hi, lo)
    arrived = exchange(part.reshape(16, 16, 128), ("y", "x"))
    lines = folded(arrived.reshape(256, 128))
    arrived = exchange(lines.reshape(32, 1, 512), ("zh", "zl", "core"))
    wave, ca, sa = phases(positions.T, mine, hi, lo)
    charge = aug_charge.reshape(171, 16 * N)
    arrived, charge, wave, ca, sa = lax.optimization_barrier((arrived, charge, wave, ca, sa))
    copies = line_part(arrived.reshape(128, 128), line_hi, line_lo)
    v = exchange(copies, "x").reshape(128, N)
    vg, part = charge_part(v, charge, wave, ca, sa)
    arrived = exchange(part.reshape(16, 1, 5632), ("y", "zl"))
    mid = met(arrived.reshape(704, 128))
    arrived = exchange(mid.reshape(4, 1, 5632), "zh")
    own = totals(arrived.reshape(176, 128))
    whole = exchange(own.reshape(16, 1, 5632), ("y", "zl"))
    return vg, jnp.moveaxis(whole.reshape(176, 4, 128)[:171], 1, 0)


def solution(mesh):
    fine = Mesh(mesh.devices.reshape(4, 4, 4, 4, 2), ("y", "zh", "zl", "x", "core"))
    placed = (P(None, FFT, GRP, None), P(), P(None, GRP), P(None, FFT, None))
    return jax.shard_map(
        body,
        mesh=fine,
        in_specs=placed,
        out_specs=(P(None, None, FFT, None), P(None, None, GRP)),
        check_vma=False,
    )
```

time: 113 us -> 107 us (0.947)
  the two profiles are of different devices: /device:TPU:32 before, /device:TPU:2 now
where the time goes in v3:
time: 107 us; the launch traced here: 106 us
  blocking collectives  68.5 us (64%)
  starting transfers between devices  14.4 us (13%)
  Pallas kernels  9.12 us (9%)
  waiting for transfers between devices  8.99 us (8%)
  local copies, waits for them, and re-layouts  4.68 us (4%)
    all_to_all x5, blocking collectives, exchange(): return lax.all_to_all(parts, axes, split_axis=0, concat_axis=0, tiled=True)  68.5 us
    all_to_all x1, starting transfers between devices, exchange(): return lax.all_to_all(parts, axes, split_axis=0, concat_axis=0, tiled=True)  14.4 us
    all_to_all x1, waiting for transfers between devices, exchange(): return lax.all_to_all(parts, axes, split_axis=0, concat_axis=0, tiled=True)  8.99 us
    pallas_call x1, Pallas kernels, plane_part(): pl.pallas_call(plane_kernel, out_shape=pltpu.VMEM((256, 128), F32), in_sp...  3.57 us
    pallas_call x1, Pallas kernels, charge_part(): pl.pallas_call(charge_kernel, out_shape=(jax.ShapeDtypeStruct((4, 2, 16,...  3.1 us
    unnamed x11, local copies, waits for them, and re-layouts  2.6 us
  transfers between devices with their start and end apart: 1, of which 1 were waited for; matrix products, arithmetic and copies ran while one was open for 4% of the time, Pallas kernels for 1%

profile of v3, /device:TPU:2, one launch (start us, length us, event | category | flops | bytes accessed | tf_op | source)
XLA Modules:
  0.0 106.4 jit_solution(4854600720544339371)
XLA Ops:
  0.6 0.0 copy-start.2
  0.6 3.6 %plane_part.1 = f32[256,128]{1,0:T(8,128)S(1)} custom-call(s32[1]{0:T(128)} %bitcast.grp_ref, f32[512,256]{1,0:T(8,128)} %bitcast.31, s32[2,1024]{1,0:T(2,128)} %mill_ref.1, bf16[256,256]{1,0:T(8,128)(2,1)} %constant.37.clone.hi_ref, bf16[256,256]{1,0:T(8,128)(2,1)} %constant.38.clone.lo_ref), custom_call_target="tpu_custom_call" | custom-call | tf_op jit(solution)/shard_map/plane_part/pallas_call | solution.py:102
  4.2 15.0 %all_to_all.30 = f32[16,16,128]{2,1,0:T(8,128)S(1)} all-to-all(f32[16,16,128]{2,1,0:T(8,128)S(1)} %bitcast.21), channel_id=1, replica_groups=mesh['y'=4,'zh'=4,'zl'=4,'x'=4,'core'=2] {'y','x'}, dimensions={0} | all-to-all | bytes 262144 | tf_op jit(solution)/shard_map/all_to_all | solution.py:270
  19.2 0.6 fold.1
  19.9 14.4 %all-to-all-start.1 = ((f32[32,1,512]{2,1,0:T(1,128)}), f32[32,1,512]{2,1,0:T(1,128)S(1)}, u32[]{:S(2)}, u32[]{:S(2)}) async-start(f32[32,1,512]{2,1,0:T(1,128)} %bitcast.4), calls=%async_computation.1 | async-start | bytes 131072 | tf_op jit(solution)/shard_map/all_to_all | solution.py:270
  34.3 0.0 copy-done.2
  34.3 0.1 pad
  34.4 0.0 copy-start.3
  34.4 0.0 copy-start
  34.4 0.0 copy-start.1
  34.4 1.7 %copy.16 = bf16[22,8,16,256]{3,1,2,0:T(8,128)(2,1)} copy(bf16[22,8,16,256]{3,2,1,0:T(8,128)(2,1)S(1)} %bitcast.29) | data formatting | bytes 2883584
  36.2 0.0 copy-done.3
  36.2 0.7 copy.12
  36.9 1.3 %constant_dynamic-slice_fusion.mill_ref = s32[2,16]{1,0:T(2,128)} fusion(s32[2,1024]{1,0:T(2,128)} %mill_ref.1, s32[]{:T(128)S(6)} %select_n.3), kind=kLoop, calls=%fused_computation.1 | loop fusion | bytes 260 | tf_op jit(solution)/shard_map/dynamic_slice | solution.py:278
  38.2 1.4 %phases.1 = (f32[128,512]{1,0:T(8,128)S(1)}, f32[128,16]{1,0:T(8,128)S(1)}, f32[128,16]{1,0:T(8,128)S(1)}) custom-call(s32[128,3]{1,0:T(8,128)} %bitcast.32, s32[2,16]{1,0:T(2,128)} %constant_dynamic-slice_fusion.mill_ref, bf16[256,256]{1,0:T(8,128)(2,1)} %constant.37.clone.hi_ref, bf16[256,256]{1,0:T(8,128)(2,1)} %constant.38.clone.lo_ref), custom_call_target="tpu_custom_call" | custom-call | tf_op jit(solution)/shard_map/phases/pallas_call | solution.py:175
  39.7 9.0 %all-to-all-done.1 = f32[32,1,512]{2,1,0:T(1,128)S(1)} async-done(((f32[32,1,512]{2,1,0:T(1,128)}), f32[32,1,512]{2,1,0:T(1,128)S(1)}, u32[]{:S(2)}, u32[]{:S(2)}) %all-to-all-start.1) | async-done | bytes 65568 | tf_op jit(solution)/shard_map/all_to_all | solution.py:270
  48.6 0.0 copy-done
  48.6 0.0 copy-done.1
  48.6 0.3 line_part.1
  49.0 8.4 %all_to_all.31 = f32[4,32,256]{2,1,0:T(8,128)S(1)} all-to-all(f32[4,32,256]{2,1,0:T(8,128)S(1)} %line_part.1), channel_id=1, replica_groups=mesh['y'=4,'zh'=4,'zl'=4,'x'=4,'core'=2] {'x'}, dimensions={0} | all-to-all | bytes 262144 | tf_op jit(solution)/shard_map/all_to_all | solution.py:270
  57.3 3.1 %charge_part.1 = (f32[4,2,16,256]{3,2,1,0:T(8,128)}, f32[704,128]{1,0:T(8,128)S(1)}) custom-call(f32[128,256]{1,0:T(8,128)S(1)} %bitcast.23, bf16[171,4096]{1,0:T(8,128)(2,1)} %bitcast.28, f32[128,512]{1,0:T(8,128)S(1)} %get-tuple-element.17.wave_ref, f32[128,16]{1,0:T(8,128)S(1)} %get-tuple-element.18.ca_ref, f32[128,16]{1,0:T(8,128)S(1)} %get-tuple-element.19.sa_ref), custom_call_target="tpu_custom_call" | custom-call | tf_op jit(solution)/shard_map/charge_part/pallas_call | solution.py:213
  60.4 14.1 %all_to_all.32 = f32[16,1,5632]{2,1,0:T(1,128)S(1)} all-to-all(f32[16,1,5632]{2,1,0:T(1,128)S(1)} %bitcast.26), channel_id=1, replica_groups=mesh['y'=4,'zh'=4,'zl'=4,'x'=4,'core'=2] {'y','zl'}, dimensions={0} | all-to-all | bytes 720896 | tf_op jit(solution)/shard_map/all_to_all | solution.py:270
  74.6 17.0 %all_to_all.33 = f32[4,1,5632]{2,1,0:T(1,128)S(1)} all-to-all(f32[4,1,5632]{2,1,0:T(1,128)S(1)} %bitcast.24), channel_id=1, replica_groups=mesh['y'=4,'zh'=4,'zl'=4,'x'=4,'core'=2] {'zh'}, dimensions={0} | all-to-all | bytes 180224 | tf_op jit(solution)/shard_map/all_to_all | solution.py:270
  91.6 14.1 %all_to_all.34 = f32[16,1,5632]{2,1,0:T(1,128)S(1)} all-to-all(f32[16,1,5632]{2,1,0:T(1,128)S(1)} %bitcast.20), channel_id=1, replica_groups=mesh['y'=4,'zh'=4,'zl'=4,'x'=4,'core'=2] {'y','zl'}, dimensions={0} | all-to-all | bytes 720896 | tf_op jit(solution)/shard_map/all_to_all | solution.py:270
  105.7 0.8 slice_bitcast_fusion
  (2 shorter events, 0.1 us)
Async XLA Ops:
  0.6 33.6 %copy-start.2 = (bf16[171,16,256]{2,1,0:T(8,128)(2,1)S(1)}, bf16[171,16,256]{2,1,0:T(8,128)(2,1)}, u32[]{:S(2)}) copy-start(bf16[171,16,256]{2,1,0:T(8,128)(2,1)} %param.11) | copy-start | bytes 4202500
  19.9 28.8 %all-to-all-start.1 = ((f32[32,1,512]{2,1,0:T(1,128)}), f32[32,1,512]{2,1,0:T(1,128)S(1)}, u32[]{:S(2)}, u32[]{:S(2)}) async-start(f32[32,1,512]{2,1,0:T(1,128)} %bitcast.4), calls=%async_computation.1 | async-start | bytes 131072 | tf_op jit(solution)/shard_map/all_to_all | solution.py:270
  34.4 1.8 %copy-start.3 = (s32[3,128]{1,0:T(4,128)S(1)}, s32[3,128]{1,0:T(4,128)}, u32[]{:S(2)}) copy-start(s32[3,128]{1,0:T(4,128)} %param.10) | copy-start | bytes 4612
  34.4 14.3 %copy-start = (bf16[256,512]{1,0:T(8,128)(2,1)S(1)}, bf16[256,512]{1,0:T(8,128)(2,1)}, u32[]{:S(2)}) copy-start(bf16[256,512]{1,0:T(8,128)(2,1)} %constant.39.clone.hi_ref) | copy-start | bytes 786436
  34.4 14.2 %copy-start.1 = (bf16[256,512]{1,0:T(8,128)(2,1)S(1)}, bf16[256,512]{1,0:T(8,128)(2,1)}, u32[]{:S(2)}) copy-start(bf16[256,512]{1,0:T(8,128)(2,1)} %constant.40.clone.lo_ref) | copy-start | bytes 786436

commit v4 on v3

v4 whole, which is shorter than its diff:
```python
import math

import jax
import jax.numpy as jnp
import numpy as np
from jax import lax
from jax.experimental import pallas as pl
from jax.experimental.pallas import tpu as pltpu
from jax.sharding import Mesh
from jax.sharding import PartitionSpec as P

N = 256
H = 128
GRP = ("x", "core")
FFT = ("y", "zh", "zl")
F32 = jnp.float32
BF16 = jnp.bfloat16
VMEM = pl.BlockSpec(memory_space=pltpu.VMEM)


def split_table(table):
    high = table.astype(np.float32).astype(jnp.bfloat16)
    low = (table - high.astype(np.float64)).astype(np.float32).astype(jnp.bfloat16)
    return high, low


def wave_table(left, right):
    angle = 2.0 * math.pi / N * np.mod(np.outer(left, right), N)
    return np.concatenate([np.cos(angle), np.sin(angle)], axis=1)


def tables():
    index = np.arange(N)
    flat = split_table(wave_table(index, index[:H]))
    z4, f = np.meshgrid(np.arange(4), np.arange(64), indexing="ij")
    plane = (f * 4 + z4).reshape(-1)
    line = split_table(wave_table(plane, index - N // 2) * float(N) ** -1.5)
    return flat, line


def split_value(x):
    high = x.astype(BF16)
    return high, (x - high.astype(F32)).astype(BF16)


def dot(a, b):
    return jnp.dot(a, b, preferred_element_type=F32)


def near(x):
    return pltpu.with_memory_space_constraint(x, pltpu.VMEM)


def picks(index):
    grid = lax.broadcasted_iota(jnp.int32, (H, 1024), 0)
    hit = grid == jnp.abs(index)
    even = jnp.where(hit, 1.0, 0.0).astype(BF16)
    odd = jnp.where(hit, jnp.where(index < 0, -1.0, 1.0), 0.0).astype(BF16)
    return jnp.concatenate([even, even], axis=0), jnp.concatenate([odd, odd], axis=0)


def place(axes):
    return lax.axis_index(axes)


def plane_kernel(pot_ref, mill_ref, pos_ref, hi_ref, lo_ref, out_ref, wave_ref, cos_ref, sin_ref, *scratch):
    pot, mill, pos, hi, lo, chosen, turned, sems = scratch
    loads = [
        pltpu.make_async_copy(mill_ref, mill, sems.at[0]),
        pltpu.make_async_copy(pos_ref, pos, sems.at[1]),
        pltpu.make_async_copy(hi_ref, hi, sems.at[2]),
        pltpu.make_async_copy(lo_ref, lo, sems.at[3]),
    ]
    chunks = [
        pltpu.make_async_copy(pot_ref.at[:, pl.ds(8 * q, 8), pl.ds(h * H, H)], pot.at[q, h], sems.at[4 + 2 * q + h])
        for q in range(4)
        for h in range(2)
    ]
    for load in loads + chunks:
        load.start()
    grp = place(GRP)
    fft = place(FFT)
    loads[0].wait()
    even_x, odd_x = picks(mill[0:1, :])
    even_y, odd_y = picks(mill[1:2, :])
    loads[1].wait()
    cols = jnp.concatenate([pos[...].astype(F32), jnp.zeros((125, 128), F32)], axis=0).T
    block = pl.multiple_of((fft >> 3) * 128, 128)
    shift = (128 - (fft & 7) * 16) & 127
    near_mill = jnp.concatenate([mill[:, pl.ds(block, 128)].astype(F32), jnp.zeros((6, 128), F32)], axis=0)
    mine = pltpu.roll(near_mill, shift, 1)
    k = (cols[:, 0:1] * mine[0:1, :] + cols[:, 1:2] * mine[1:2, :]).astype(jnp.int32)
    angle = (2.0 * math.pi / N) * jnp.bitwise_and(k, N - 1).astype(F32)
    cos_ref[...] = jnp.cos(angle)
    sin_ref[...] = jnp.sin(angle)
    zcol = cols[:, 2:3].astype(jnp.int32)
    grid = lax.broadcasted_iota(jnp.int32, (128, N), 1)
    pick = jnp.where(grid == zcol, 1.0, 0.0).astype(BF16)
    sign = 1.0 - 2.0 * jnp.bitwise_and(zcol, 1).astype(F32)
    loads[2].wait()
    loads[3].wait()
    wave = dot(pick, hi[...]) + dot(pick, lo[...])
    turn = wave * sign
    wave_ref[:, 0:H] = turn[:, :H]
    wave_ref[:, H:N] = wave[:, :H]
    wave_ref[:, N : N + H] = turn[:, H:]
    wave_ref[:, N + H :] = wave[:, H:]

    start = pl.multiple_of(grp * 32, 32)
    near_hi = hi[pl.ds(start, 32), :]
    near_lo = lo[pl.ds(start, 32), :]
    cos_y = dot(jnp.concatenate([near_hi[:, :H], near_lo[:, :H]], axis=1), even_y)
    sin_y = dot(jnp.concatenate([near_hi[:, H:], near_lo[:, H:]], axis=1), odd_y)
    wide = jnp.concatenate([hi[...], lo[...], hi[...]], axis=0)
    for q in range(4):
        halves = []
        for h in range(2):
            chunks[2 * q + h].wait()
            rows = pot.at[q, h].reshape(128, H)
            halves.append(jnp.concatenate([rows[pl.ds(y, 16, 8), :] for y in range(8)], axis=0))
        x = jnp.concatenate(halves, axis=1)
        p_hi, p_lo = split_value(x)
        w_hi, w_lo = split_value(dot(jnp.concatenate([p_hi, p_hi, p_lo], axis=1), wide))
        at = q * 128
        chosen[0, at : at + 128, 0:H] = w_hi[:, :H]
        chosen[0, at : at + 128, H:N] = w_lo[:, :H]
        chosen[1, at : at + 128, 0:H] = w_hi[:, H:]
        chosen[1, at : at + 128, H:N] = w_lo[:, H:]
    for b in range(4):
        at = b * N
        even = dot(chosen[0], even_x[:, at : at + N])
        odd = dot(chosen[1], odd_x[:, at : at + N])
        real = jnp.zeros((16, N), F32)
        imag = jnp.zeros((16, N), F32)
        for y in range(32):
            e = even[y * 16 : (y + 1) * 16, :]
            o = odd[y * 16 : (y + 1) * 16, :]
            cy = cos_y[y : y + 1, at : at + N]
            sy = sin_y[y : y + 1, at : at + N]
            real = real + (e * cy - o * sy)
            imag = imag - (e * sy + o * cy)
        for h in range(2):
            part = jnp.concatenate([real[:, h * H : (h + 1) * H], imag[:, h * H : (h + 1) * H]], axis=0)
            turned[at + h * H : at + (h + 1) * H, :] = jnp.concatenate([part] * 4, axis=0).T
    lane = lax.broadcasted_iota(jnp.int32, (16, 128), 1)
    for y in range(4):
        for x in range(4):
            base = y * 256 + x * 4
            parts = [turned[pl.ds(base + j, 16, 16), :] for j in range(4)]
            low = jnp.where(lane < 32, parts[0], parts[1])
            high = jnp.where(lane < 96, parts[2], parts[3])
            at = (y * 4 + x) * 16
            out_ref[at : at + 16, :] = jnp.where(lane < 64, low, high)


def plane_part(potential, stick_mill, positions, hi, lo):
    return pl.pallas_call(
        plane_kernel,
        out_shape=(
            pltpu.VMEM((256, 128), F32),
            pltpu.VMEM((128, 2 * N), F32),
            pltpu.VMEM((128, 128), F32),
            pltpu.VMEM((128, 128), F32),
        ),
        in_specs=[pl.BlockSpec(memory_space=pl.ANY)] * 5,
        out_specs=(VMEM,) * 4,
        scratch_shapes=[
            pltpu.VMEM((4, 2, 16, 8, H), F32),
            pltpu.VMEM((2, 1024), jnp.int32),
            pltpu.VMEM((3, 128), jnp.int32),
            pltpu.VMEM((N, N), BF16),
            pltpu.VMEM((N, N), BF16),
            pltpu.VMEM((2, 512, N), BF16),
            pltpu.VMEM((1024, 128), F32),
            pltpu.SemaphoreType.DMA((12,)),
        ],
        name="plane_part",
    )(potential, stick_mill, positions, hi, lo)


def fold_kernel(in_ref, out_ref):
    for y in range(4):
        at = y * 64
        total = (in_ref[at : at + 16, :] + in_ref[at + 16 : at + 32, :]) + (
            in_ref[at + 32 : at + 48, :] + in_ref[at + 48 : at + 64, :]
        )
        for core in range(2):
            out_ref[pl.ds(core * 4 + y, 16, 8), :] = total


def folded(arrived):
    return pl.pallas_call(
        fold_kernel,
        out_shape=pltpu.VMEM((128, 128), F32),
        in_specs=[VMEM],
        out_specs=VMEM,
        name="fold",
    )(near(arrived))


def line_kernel(in_ref, hi_ref, lo_ref, out_ref, turned):
    rows = [in_ref[pl.ds(y, 16, 8), :] + in_ref[pl.ds(y + 4, 16, 8), :] for y in range(4)]
    turned[...] = jnp.concatenate(rows + rows, axis=0).T
    lower = lax.broadcasted_iota(jnp.int32, (32, 128), 1) < 64
    halves = [jnp.where(lower, turned[pl.ds(2 * b, 32, 4), :], turned[pl.ds(2 * b + 1, 32, 4), :]) for b in range(2)]
    a_hi, a_lo = split_value(jnp.concatenate(halves, axis=1))
    hi = hi_ref[...]
    r = dot(a_hi, hi) + dot(a_hi, lo_ref[...]) + dot(a_lo, hi)
    first = lax.broadcasted_iota(jnp.int32, (8, N), 0) < 4
    for j in range(4):
        own = r[j * 8 : j * 8 + 8, :N]
        other = pltpu.roll(r[j * 8 : j * 8 + 8, N:], 4, 0)
        v = own + jnp.where(first, other, -other)
        for x in range(4):
            out_ref[x, j * 8 : j * 8 + 8, :] = v


def line_part(arrived, hi, lo):
    return pl.pallas_call(
        line_kernel,
        out_shape=pltpu.VMEM((4, 32, N), F32),
        in_specs=[VMEM] * 3,
        out_specs=VMEM,
        scratch_shapes=[pltpu.VMEM((128, 128), F32)],
        name="line_part",
    )(near(arrived), near(hi), near(lo))


def charge_kernel(v_ref, q_ref, wave_ref, ca_ref, sa_ref, vg_ref, d_ref, mixed):
    for s in range(16):
        top = s * 8
        for c in range(4):
            vg_ref[c, 0, s : s + 1, :] = v_ref[top + c : top + c + 1, :]
            vg_ref[c, 1, s : s + 1, :] = v_ref[top + 4 + c : top + 5 + c, :]
        for a in range(0, 128, 16):
            ca = ca_ref[a : a + 16, s : s + 1]
            sa = sa_ref[a : a + 16, s : s + 1]
            cb = wave_ref[a : a + 16, :N]
            sb = wave_ref[a : a + 16, N:]
            cosine = ca * cb - sa * sb
            sine = sa * cb + ca * sb
            for c in range(4):
                real = v_ref[top + c : top + c + 1, :]
                imag = v_ref[top + 4 + c : top + 5 + c, :]
                mixed[c * 128 + a : c * 128 + a + 16, s * N : (s + 1) * N] = (real * cosine - imag * sine).astype(BF16)
    d = lax.dot_general(q_ref[...], mixed[...], (((1,), (1,)), ((), ())), preferred_element_type=F32)
    for c in range(4):
        d_ref[pl.ds(c, 171, 4), :] = d[:, c * 128 : (c + 1) * 128]
    d_ref[684:704, :] = jnp.zeros((20, 128), F32)


def charge_part(v, charge, wave, ca, sa):
    return pl.pallas_call(
        charge_kernel,
        out_shape=(jax.ShapeDtypeStruct((4, 2, 16, N), F32), pltpu.VMEM((704, 128), F32)),
        in_specs=[VMEM] * 5,
        out_specs=(VMEM,) * 2,
        scratch_shapes=[pltpu.VMEM((512, 4096), BF16)],
        name="charge_part",
    )(near(v), near(charge), near(wave), near(ca), near(sa))


def meet_kernel(in_ref, out_ref, half):
    total = in_ref[0:88, :]
    for m in range(1, 8):
        total = total + in_ref[m * 88 : (m + 1) * 88, :]
    half[...] = total
    own = half[0:44, :] + half[44:88, :]
    for m in range(4):
        out_ref[m * 44 : (m + 1) * 44, :] = own


def met(arrived):
    return pl.pallas_call(
        meet_kernel,
        out_shape=pltpu.VMEM((176, 128), F32),
        in_specs=[VMEM],
        out_specs=VMEM,
        scratch_shapes=[pltpu.VMEM((88, 128), F32)],
        name="meet",
    )(near(arrived))


def total_kernel(in_ref, out_ref, half):
    half[...] = in_ref[0:88, :] + in_ref[88:176, :]
    own = half[0:44, :] + half[44:88, :]
    half[0:44, :] = own
    half[44:88, :] = own
    pair = half[...]
    for m in range(8):
        out_ref[m * 88 : (m + 1) * 88, :] = pair


def totals(arrived):
    return pl.pallas_call(
        total_kernel,
        out_shape=pltpu.VMEM((704, 128), F32),
        in_specs=[VMEM],
        out_specs=VMEM,
        scratch_shapes=[pltpu.VMEM((88, 128), F32)],
        name="totals",
    )(near(arrived))


def exchange(parts, axes):
    return lax.all_to_all(parts, axes, split_axis=0, concat_axis=0, tiled=True)


def body(potential, stick_mill, positions, aug_charge):
    (hi, lo), (line_hi, line_lo) = tables()
    hi, lo, line_hi, line_lo = map(jnp.asarray, (hi, lo, line_hi, line_lo))
    part, wave, ca, sa = plane_part(potential.reshape(16, 32, N), stick_mill, positions, hi, lo)
    arrived = exchange(part.reshape(16, 16, 128), ("y", "x"))
    lines = folded(arrived.reshape(256, 128))
    arrived = exchange(lines.reshape(32, 1, 512), ("zh", "zl", "core"))
    copies = line_part(arrived.reshape(128, 128), line_hi, line_lo)
    v = exchange(copies, "x").reshape(128, N)
    v, aug_charge = lax.optimization_barrier((v, aug_charge))
    charge = aug_charge.reshape(171, 16 * N)
    vg, part = charge_part(v, charge, wave, ca, sa)
    arrived = exchange(part.reshape(16, 1, 5632), ("y", "zl"))
    mid = met(arrived.reshape(704, 128))
    arrived = exchange(mid.reshape(4, 1, 5632), "zh")
    own = totals(arrived.reshape(176, 128))
    whole = exchange(own.reshape(16, 1, 5632), ("y", "zl"))
    return vg, jnp.moveaxis(whole.reshape(176, 4, 128)[:171], 1, 0)


def solution(mesh):
    fine = Mesh(mesh.devices.reshape(4, 4, 4, 4, 2), ("y", "zh", "zl", "x", "core"))
    placed = (P(None, FFT, GRP, None), P(), P(None, GRP), P(None, FFT, None))
    return jax.shard_map(
        body,
        mesh=fine,
        in_specs=placed,
        out_specs=(P(None, None, FFT, None), P(None, None, GRP)),
        check_vma=False,
    )
```

time: 107 us -> 106 us (level)
  blocking collectives: 68.5 us -> 97.1 us
  starting transfers between devices: 14.4 us -> 0 us
  waiting for transfers between devices: 8.99 us -> 0 us
  local copies, waits for them, and re-layouts: 4.68 us -> 1.5 us
  Pallas kernels: 9.12 us -> 6.6 us
    all_to_all x5 -> x6, blocking collectives: 68.5 us -> 97.1 us  [exchange(): return lax.all_to_all(parts, axes, split_axis=0, concat_axis=0, tiled=True)]
    all_to_all x1 -> x0, starting transfers between devices: 14.4 us -> none  [exchange(): return lax.all_to_all(parts, axes, split_axis=0, concat_axis=0, tiled=True)]
    all_to_all x1 -> x0, waiting for transfers between devices: 8.99 us -> none  [exchange(): return lax.all_to_all(parts, axes, split_axis=0, concat_axis=0, tiled=True)]
    unnamed x11 -> x8, local copies, waits for them, and re-layouts: 2.6 us -> 0.75 us
    dynamic_slice x1 -> x0, local copies, waits for them, and re-layouts: 1.32 us -> none  [body(): mine = lax.dynamic_slice_in_dim(stick_mill, fft * 16, 16, 1)]
    pallas_call x2 -> x1, Pallas kernels: 5 us -> 3.78 us  [plane_part(): pl.pallas_call(plane_kernel, out_shape=(pltpu.VMEM((256, 128), F32), pltp...]
  transfers between devices with their start and end apart: 1 -> 0, of which waited for: 1 -> 0; matrix products, arithmetic and copies ran while one was open for 4% -> 0% of each run, Pallas kernels for 1% -> 0%
where the time goes in v4:
time: 106 us
  blocking collectives  97.1 us (92%)
  Pallas kernels  6.6 us (6%)
  local copies, waits for them, and re-layouts  1.5 us (1%)
    all_to_all x6, blocking collectives, exchange(): return lax.all_to_all(parts, axes, split_axis=0, concat_axis=0, tiled=True)  97.1 us
    pallas_call x1, Pallas kernels, plane_part(): pl.pallas_call(plane_kernel, out_shape=(pltpu.VMEM((256, 128), F32), pltp...  3.78 us
    pallas_call x1, Pallas kernels, charge_part(): pl.pallas_call(charge_kernel, out_shape=(jax.ShapeDtypeStruct((4, 2, 16,...  2.45 us

profile of v4, /device:TPU:2, one launch (start us, length us, event | category | flops | bytes accessed | tf_op | source)
XLA Modules:
  0.0 105.9 jit_solution(9159623282415152909)
XLA Ops:
  0.6 0.0 copy-start
  0.6 0.0 copy-start.1
  0.7 0.0 copy-start.2
  0.7 3.8 %plane_part.1 = (f32[256,128]{1,0:T(8,128)S(1)}, f32[128,512]{1,0:T(8,128)S(1)}, f32[128,128]{1,0:T(8,128)S(1)}, f32[128,128]{1,0:T(8,128)S(1)}) custom-call(f32[16,32,256]{2,1,0:T(8,128)} %bitcast.30, s32[2,1024]{1,0:T(2,128)} %mill_ref.1, s32[3,128]{1,0:T(4,128)} %pos_ref.1, bf16[256,256]{1,0:T(8,128)(2,1)} %constant.8.clone.hi_ref, ...), custom_call_target="tpu_custom_call" | custom-call | tf_op jit(solution)/shard_map/plane_part/pallas_call | solution.py:157
  4.5 15.0 %all_to_all.30 = f32[16,16,128]{2,1,0:T(8,128)S(1)} all-to-all(f32[16,16,128]{2,1,0:T(8,128)S(1)} %bitcast.27), channel_id=1, replica_groups=mesh['y'=4,'zh'=4,'zl'=4,'x'=4,'core'=2] {'y','x'}, dimensions={0} | all-to-all | bytes 262144 | tf_op jit(solution)/shard_map/all_to_all | solution.py:306
  19.5 28.6 %all_to_all.31 = f32[32,1,512]{2,1,0:T(1,128)S(1)} all-to-all(f32[32,1,512]{2,1,0:T(1,128)S(1)} %bitcast.25), channel_id=1, replica_groups=mesh['y'=4,'zh'=4,'zl'=4,'x'=4,'core'=2] {'zh','zl','core'}, dimensions={0} | all-to-all | bytes 131072 | tf_op jit(solution)/shard_map/all_to_all | solution.py:306
  48.0 0.0 copy-done
  48.0 0.0 copy-done.1
  48.0 0.3 line_part.1
  48.3 8.4 %all_to_all.32 = f32[4,32,256]{2,1,0:T(8,128)S(1)} all-to-all(f32[4,32,256]{2,1,0:T(8,128)S(1)} %line_part.1), channel_id=1, replica_groups=mesh['y'=4,'zh'=4,'zl'=4,'x'=4,'core'=2] {'x'}, dimensions={0} | all-to-all | bytes 262144 | tf_op jit(solution)/shard_map/all_to_all | solution.py:306
  56.7 0.0 copy-done.2
  56.7 0.1 pad
  56.8 0.6 copy.14
  57.4 2.4 %charge_part.1 = (f32[4,2,16,256]{3,2,1,0:T(8,128)}, f32[704,128]{1,0:T(8,128)S(1)}) custom-call(f32[128,256]{1,0:T(8,128)S(1)} %bitcast.21, bf16[171,4096]{1,0:T(8,128)(2,1)S(1)} %bitcast.17, f32[128,512]{1,0:T(8,128)S(1)} %get-tuple-element.13.wave_ref, f32[128,128]{1,0:T(8,128)S(1)} %get-tuple-element.14.ca_ref, f32[128,128]{1,0:T(8,128)S(1)} %get-tuple-element.15.sa_ref), custom_call_target="tpu_custom_call" | custom-call | tf_op jit(solution)/shard_map/charge_part/pallas_call | solution.py:253
  59.9 14.1 %all_to_all.33 = f32[16,1,5632]{2,1,0:T(1,128)S(1)} all-to-all(f32[16,1,5632]{2,1,0:T(1,128)S(1)} %bitcast.24), channel_id=1, replica_groups=mesh['y'=4,'zh'=4,'zl'=4,'x'=4,'core'=2] {'y','zl'}, dimensions={0} | all-to-all | bytes 720896 | tf_op jit(solution)/shard_map/all_to_all | solution.py:306
  74.0 17.0 %all_to_all.34 = f32[4,1,5632]{2,1,0:T(1,128)S(1)} all-to-all(f32[4,1,5632]{2,1,0:T(1,128)S(1)} %bitcast.22), channel_id=1, replica_groups=mesh['y'=4,'zh'=4,'zl'=4,'x'=4,'core'=2] {'zh'}, dimensions={0} | all-to-all | bytes 180224 | tf_op jit(solution)/shard_map/all_to_all | solution.py:306
  91.0 14.1 %all_to_all.35 = f32[16,1,5632]{2,1,0:T(1,128)S(1)} all-to-all(f32[16,1,5632]{2,1,0:T(1,128)S(1)} %bitcast.19), channel_id=1, replica_groups=mesh['y'=4,'zh'=4,'zl'=4,'x'=4,'core'=2] {'y','zl'}, dimensions={0} | all-to-all | bytes 720896 | tf_op jit(solution)/shard_map/all_to_all | solution.py:306
  105.1 0.8 slice_bitcast_fusion
  (3 shorter events, 0.1 us)
Async XLA Ops:
  0.6 47.4 %copy-start = (bf16[256,512]{1,0:T(8,128)(2,1)S(1)}, bf16[256,512]{1,0:T(8,128)(2,1)}, u32[]{:S(2)}) copy-start(bf16[256,512]{1,0:T(8,128)(2,1)} %constant.11.clone.lo_ref) | copy-start | bytes 786436
  0.6 47.4 %copy-start.1 = (bf16[256,512]{1,0:T(8,128)(2,1)S(1)}, bf16[256,512]{1,0:T(8,128)(2,1)}, u32[]{:S(2)}) copy-start(bf16[256,512]{1,0:T(8,128)(2,1)} %constant.10.clone.hi_ref) | copy-start | bytes 786436
  0.7 56.0 %copy-start.2 = (bf16[171,16,256]{2,1,0:T(8,128)(2,1)S(1)}, bf16[171,16,256]{2,1,0:T(8,128)(2,1)}, u32[]{:S(2)}) copy-start(bf16[171,16,256]{2,1,0:T(8,128)(2,1)} %param.11) | copy-start | bytes 4202500

commit v5 on v4

--- a/solution.py
+++ b/solution.py
@@ -33,6 +33,7 @@
     index = np.arange(N)
     flat = split_table(wave_table(index, index[:H]))
     z4, f = np.meshgrid(np.arange(4), np.arange(64), indexing="ij")
+    f = f // 16 * 16 + (f + 8) % 16
     plane = (f * 4 + z4).reshape(-1)
     line = split_table(wave_table(plane, index - N // 2) * float(N) ** -1.5)
     return flat, line
@@ -185,7 +186,8 @@
             in_ref[at + 32 : at + 48, :] + in_ref[at + 48 : at + 64, :]
         )
         for core in range(2):
-            out_ref[pl.ds(core * 4 + y, 16, 8), :] = total
+            out_ref[pl.ds(core * 4 + y, 8, 8), :] = total[8:16, :]
+            out_ref[pl.ds(64 + core * 4 + y, 8, 8), :] = total[0:8, :]
 
 
 def folded(arrived):
@@ -302,8 +304,9 @@
     )(near(arrived))
 
 
-def exchange(parts, axes):
-    return lax.all_to_all(parts, axes, split_axis=0, concat_axis=0, tiled=True)
+def exchange(parts, axes, members=None):
+    groups = None if members is None else [members]
+    return lax.all_to_all(parts, axes, split_axis=0, concat_axis=0, tiled=True, axis_index_groups=groups)
 
 
 def body(potential, stick_mill, positions, aug_charge):
@@ -312,7 +315,7 @@
     part, wave, ca, sa = plane_part(potential.reshape(16, 32, N), stick_mill, positions, hi, lo)
     arrived = exchange(part.reshape(16, 16, 128), ("y", "x"))
     lines = folded(arrived.reshape(256, 128))
-    arrived = exchange(lines.reshape(32, 1, 512), ("zh", "zl", "core"))
+    arrived = exchange(lines.reshape(32, 1, 512), ("zh", "zl", "core"), [(i + 16) % 32 for i in range(32)])
     copies = line_part(arrived.reshape(128, 128), line_hi, line_lo)
     v = exchange(copies, "x").reshape(128, N)
     v, aug_charge = lax.optimization_barrier((v, aug_charge))
@@ -320,7 +323,7 @@
     vg, part = charge_part(v, charge, wave, ca, sa)
     arrived = exchange(part.reshape(16, 1, 5632), ("y", "zl"))
     mid = met(arrived.reshape(704, 128))
-    arrived = exchange(mid.reshape(4, 1, 5632), "zh")
+    arrived = exchange(mid.reshape(4, 1, 5632), "zh", [2, 3, 0, 1])
     own = totals(arrived.reshape(176, 128))
     whole = exchange(own.reshape(16, 1, 5632), ("y", "zl"))
     return vg, jnp.moveaxis(whole.reshape(176, 4, 128)[:171], 1, 0)

time: 106 us -> 100 us (0.943)
  blocking collectives: 97.1 us -> 91.1 us
    all_to_all x6, blocking collectives: 97.1 us -> 91.1 us  [exchange(): lax.all_to_all(parts, axes, split_axis=0, concat_axis=0, tiled=True, axis...]
where the time goes in v5:
time: 100 us; the launch traced here: 99.9 us
  blocking collectives  91.1 us (91%)
  Pallas kernels  6.6 us (7%)
  local copies, waits for them, and re-layouts  1.5 us (2%)
    all_to_all x6, blocking collectives, exchange(): lax.all_to_all(parts, axes, split_axis=0, concat_axis=0, tiled=True, axis...  91.1 us
    pallas_call x1, Pallas kernels, plane_part(): pl.pallas_call(plane_kernel, out_shape=(pltpu.VMEM((256, 128), F32), pltp...  3.78 us
    pallas_call x1, Pallas kernels, charge_part(): pl.pallas_call(charge_kernel, out_shape=(jax.ShapeDtypeStruct((4, 2, 16,...  2.45 us

profile of v5, /device:TPU:2, one launch (start us, length us, event | category | flops | bytes accessed | tf_op | source)
XLA Modules:
  0.0 99.9 jit_solution(15939150110562703093)
XLA Ops:
  0.6 0.0 copy-start
  0.6 0.0 copy-start.1
  0.7 0.0 copy-start.2
  0.7 3.8 %plane_part.1 = (f32[256,128]{1,0:T(8,128)S(1)}, f32[128,512]{1,0:T(8,128)S(1)}, f32[128,128]{1,0:T(8,128)S(1)}, f32[128,128]{1,0:T(8,128)S(1)}) custom-call(f32[16,32,256]{2,1,0:T(8,128)} %bitcast.30, s32[2,1024]{1,0:T(2,128)} %mill_ref.1, s32[3,128]{1,0:T(4,128)} %pos_ref.1, bf16[256,256]{1,0:T(8,128)(2,1)} %constant.8.clone.hi_ref, ...), custom_call_target="tpu_custom_call" | custom-call | tf_op jit(solution)/shard_map/plane_part/pallas_call | solution.py:158
  4.5 15.0 %all_to_all.30 = f32[16,16,128]{2,1,0:T(8,128)S(1)} all-to-all(f32[16,16,128]{2,1,0:T(8,128)S(1)} %bitcast.27), channel_id=1, replica_groups=mesh['y'=4,'zh'=4,'zl'=4,'x'=4,'core'=2] {'y','x'}, dimensions={0} | all-to-all | bytes 262144 | tf_op jit(solution)/shard_map/all_to_all | solution.py:309
  19.5 22.1 %all_to_all.31 = f32[32,1,512]{2,1,0:T(1,128)S(1)} all-to-all(f32[32,1,512]{2,1,0:T(1,128)S(1)} %bitcast.25), channel_id=1, replica_groups={{64,65,72,73,80,81,88,89,96,97,104,105,112,113,120,121,0,1,8,9,16,17,24..., dimensions={0} | all-to-all | bytes 131072 | tf_op jit(solution)/shard_map/all_to_all | solution.py:309
  41.5 0.0 copy-done
  41.5 0.0 copy-done.1
  41.5 0.3 line_part.1
  41.8 8.4 %all_to_all.32 = f32[4,32,256]{2,1,0:T(8,128)S(1)} all-to-all(f32[4,32,256]{2,1,0:T(8,128)S(1)} %line_part.1), channel_id=1, replica_groups=mesh['y'=4,'zh'=4,'zl'=4,'x'=4,'core'=2] {'x'}, dimensions={0} | all-to-all | bytes 262144 | tf_op jit(solution)/shard_map/all_to_all | solution.py:309
  50.2 0.0 copy-done.2
  50.2 0.1 pad
  50.3 0.6 copy.14
  50.9 2.4 %charge_part.1 = (f32[4,2,16,256]{3,2,1,0:T(8,128)}, f32[704,128]{1,0:T(8,128)S(1)}) custom-call(f32[128,256]{1,0:T(8,128)S(1)} %bitcast.21, bf16[171,4096]{1,0:T(8,128)(2,1)S(1)} %bitcast.17, f32[128,512]{1,0:T(8,128)S(1)} %get-tuple-element.13.wave_ref, f32[128,128]{1,0:T(8,128)S(1)} %get-tuple-element.14.ca_ref, f32[128,128]{1,0:T(8,128)S(1)} %get-tuple-element.15.sa_ref), custom_call_target="tpu_custom_call" | custom-call | tf_op jit(solution)/shard_map/charge_part/pallas_call | solution.py:255
  53.4 16.5 %all_to_all.33 = f32[16,1,5632]{2,1,0:T(1,128)S(1)} all-to-all(f32[16,1,5632]{2,1,0:T(1,128)S(1)} %bitcast.24), channel_id=1, replica_groups=mesh['y'=4,'zh'=4,'zl'=4,'x'=4,'core'=2] {'y','zl'}, dimensions={0} | all-to-all | bytes 720896 | tf_op jit(solution)/shard_map/all_to_all | solution.py:309
  69.9 15.0 %all_to_all.34 = f32[4,1,5632]{2,1,0:T(1,128)S(1)} all-to-all(f32[4,1,5632]{2,1,0:T(1,128)S(1)} %bitcast.22), channel_id=1, replica_groups={{64,96,0,32},{65,97,1,33},{66,98,2,34},{67,99,3,35},{68,100,4,36},{69,1..., dimensions={0} | all-to-all | bytes 180224 | tf_op jit(solution)/shard_map/all_to_all | solution.py:309
  84.9 14.2 %all_to_all.35 = f32[16,1,5632]{2,1,0:T(1,128)S(1)} all-to-all(f32[16,1,5632]{2,1,0:T(1,128)S(1)} %bitcast.19), channel_id=1, replica_groups=mesh['y'=4,'zh'=4,'zl'=4,'x'=4,'core'=2] {'y','zl'}, dimensions={0} | all-to-all | bytes 720896 | tf_op jit(solution)/shard_map/all_to_all | solution.py:309
  99.1 0.8 slice_bitcast_fusion
  (3 shorter events, 0.1 us)
Async XLA Ops:
  0.6 40.9 %copy-start = (bf16[256,512]{1,0:T(8,128)(2,1)S(1)}, bf16[256,512]{1,0:T(8,128)(2,1)}, u32[]{:S(2)}) copy-start(bf16[256,512]{1,0:T(8,128)(2,1)} %constant.11.clone.lo_ref) | copy-start | bytes 786436
  0.6 40.9 %copy-start.1 = (bf16[256,512]{1,0:T(8,128)(2,1)S(1)}, bf16[256,512]{1,0:T(8,128)(2,1)}, u32[]{:S(2)}) copy-start(bf16[256,512]{1,0:T(8,128)(2,1)} %constant.10.clone.hi_ref) | copy-start | bytes 786436
  0.7 49.5 %copy-start.2 = (bf16[171,16,256]{2,1,0:T(8,128)(2,1)S(1)}, bf16[171,16,256]{2,1,0:T(8,128)(2,1)}, u32[]{:S(2)}) copy-start(bf16[171,16,256]{2,1,0:T(8,128)(2,1)} %param.11) | copy-start | bytes 4202500

commit v6 on v4

--- a/solution.py
+++ b/solution.py
@@ -17,6 +17,13 @@
 BF16 = jnp.bfloat16
 VMEM = pl.BlockSpec(memory_space=pltpu.VMEM)
 
+FIRST = 10
+LINE = [2 * ((FIRST + i) % 16) + core for i in range(16) for core in (1, 0)]
+FAR = [[1, 6, 8, 12], [0, 5, 9, 14], [2, 4, 10, 15], [3, 7, 11, 13]]
+LEADS = [8, 9, 10, 11]
+NEAR = [[16 * y + four[b] for four in FAR for y in range(4)] for b in range(4)]
+CROSS = [[16 * y + z for z in [lead] + [z for z in four if z != lead]] for four, lead in zip(FAR, LEADS) for y in range(4)]
+
 
 def split_table(table):
     high = table.astype(np.float32).astype(jnp.bfloat16)
@@ -33,6 +40,7 @@
     index = np.arange(N)
     flat = split_table(wave_table(index, index[:H]))
     z4, f = np.meshgrid(np.arange(4), np.arange(64), indexing="ij")
+    f = f // 16 * 16 + (f + FIRST) % 16
     plane = (f * 4 + z4).reshape(-1)
     line = split_table(wave_table(plane, index - N // 2) * float(N) ** -1.5)
     return flat, line
@@ -45,6 +53,24 @@
 
 def dot(a, b):
     return jnp.dot(a, b, preferred_element_type=F32)
+
+
+def fitted(values, degree=8):
+    fit = np.polynomial.chebyshev.Chebyshev.interpolate(lambda w: values(np.sqrt(w)), degree, domain=[0.0, 1.0])
+    return [float(c) for c in fit.convert(kind=np.polynomial.Polynomial).coef]
+
+
+def turn_of(k):
+    u = (k - H).astype(F32) * (1.0 / H)
+    w = u * u
+    even = fitted(lambda r: -np.cos(math.pi * r))
+    odd = fitted(lambda r: -math.pi * np.sinc(r))
+    cosine = jnp.full_like(u, even[-1])
+    sine = jnp.full_like(u, odd[-1])
+    for e, o in zip(even[-2::-1], odd[-2::-1]):
+        cosine = cosine * w + e
+        sine = sine * w + o
+    return cosine, sine * u
 
 
 def near(x):
@@ -90,9 +116,7 @@
     near_mill = jnp.concatenate([mill[:, pl.ds(block, 128)].astype(F32), jnp.zeros((6, 128), F32)], axis=0)
     mine = pltpu.roll(near_mill, shift, 1)
     k = (cols[:, 0:1] * mine[0:1, :] + cols[:, 1:2] * mine[1:2, :]).astype(jnp.int32)
-    angle = (2.0 * math.pi / N) * jnp.bitwise_and(k, N - 1).astype(F32)
-    cos_ref[...] = jnp.cos(angle)
-    sin_ref[...] = jnp.sin(angle)
+    cos_ref[...], sin_ref[...] = turn_of(jnp.bitwise_and(k, N - 1))
     zcol = cols[:, 2:3].astype(jnp.int32)
     grid = lax.broadcasted_iota(jnp.int32, (128, N), 1)
     pick = jnp.where(grid == zcol, 1.0, 0.0).astype(BF16)
@@ -184,6 +208,7 @@
         total = (in_ref[at : at + 16, :] + in_ref[at + 16 : at + 32, :]) + (
             in_ref[at + 32 : at + 48, :] + in_ref[at + 48 : at + 64, :]
         )
+        total = pltpu.roll(total, 16 - FIRST, 0)
         for core in range(2):
             out_ref[pl.ds(core * 4 + y, 16, 8), :] = total
 
@@ -226,12 +251,16 @@
     )(near(arrived), near(hi), near(lo))
 
 
-def charge_kernel(v_ref, q_ref, wave_ref, ca_ref, sa_ref, vg_ref, d_ref, mixed):
+def charge_kernel(v_ref, q_ref, wave_ref, ca_ref, sa_ref, vg_out, d_ref, mixed, vg_ref, sem):
     for s in range(16):
         top = s * 8
         for c in range(4):
             vg_ref[c, 0, s : s + 1, :] = v_ref[top + c : top + c + 1, :]
             vg_ref[c, 1, s : s + 1, :] = v_ref[top + 4 + c : top + 5 + c, :]
+    save = pltpu.make_async_copy(vg_ref, vg_out, sem)
+    save.start()
+    for s in range(16):
+        top = s * 8
         for a in range(0, 128, 16):
             ca = ca_ref[a : a + 16, s : s + 1]
             sa = sa_ref[a : a + 16, s : s + 1]
@@ -247,6 +276,7 @@
     for c in range(4):
         d_ref[pl.ds(c, 171, 4), :] = d[:, c * 128 : (c + 1) * 128]
     d_ref[684:704, :] = jnp.zeros((20, 128), F32)
+    save.wait()
 
 
 def charge_part(v, charge, wave, ca, sa):
@@ -254,8 +284,12 @@
         charge_kernel,
         out_shape=(jax.ShapeDtypeStruct((4, 2, 16, N), F32), pltpu.VMEM((704, 128), F32)),
         in_specs=[VMEM] * 5,
-        out_specs=(VMEM,) * 2,
-        scratch_shapes=[pltpu.VMEM((512, 4096), BF16)],
+        out_specs=(pl.BlockSpec(memory_space=pl.ANY), VMEM),
+        scratch_shapes=[
+            pltpu.VMEM((512, 4096), BF16),
+            pltpu.VMEM((4, 2, 16, N), F32),
+            pltpu.SemaphoreType.DMA(()),
+        ],
         name="charge_part",
     )(near(v), near(charge), near(wave), near(ca), near(sa))
 
@@ -302,8 +336,8 @@
     )(near(arrived))
 
 
-def exchange(parts, axes):
-    return lax.all_to_all(parts, axes, split_axis=0, concat_axis=0, tiled=True)
+def exchange(parts, axes, groups=None):
+    return lax.all_to_all(parts, axes, split_axis=0, concat_axis=0, tiled=True, axis_index_groups=groups)
 
 
 def body(potential, stick_mill, positions, aug_charge):
@@ -312,17 +346,17 @@
     part, wave, ca, sa = plane_part(potential.reshape(16, 32, N), stick_mill, positions, hi, lo)
     arrived = exchange(part.reshape(16, 16, 128), ("y", "x"))
     lines = folded(arrived.reshape(256, 128))
-    arrived = exchange(lines.reshape(32, 1, 512), ("zh", "zl", "core"))
+    arrived = exchange(lines.reshape(32, 1, 512), ("zh", "zl", "core"), [LINE])
     copies = line_part(arrived.reshape(128, 128), line_hi, line_lo)
     v = exchange(copies, "x").reshape(128, N)
     v, aug_charge = lax.optimization_barrier((v, aug_charge))
     charge = aug_charge.reshape(171, 16 * N)
     vg, part = charge_part(v, charge, wave, ca, sa)
-    arrived = exchange(part.reshape(16, 1, 5632), ("y", "zl"))
+    arrived = exchange(part.reshape(16, 1, 5632), FFT, NEAR)
     mid = met(arrived.reshape(704, 128))
-    arrived = exchange(mid.reshape(4, 1, 5632), "zh")
+    arrived = exchange(mid.reshape(4, 1, 5632), FFT, CROSS)
     own = totals(arrived.reshape(176, 128))
-    whole = exchange(own.reshape(16, 1, 5632), ("y", "zl"))
+    whole = exchange(own.reshape(16, 1, 5632), FFT, NEAR)
     return vg, jnp.moveaxis(whole.reshape(176, 4, 128)[:171], 1, 0)
 
 

time: 106 us -> 97 us (0.915)
  the two profiles are of different devices: /device:TPU:2 before, /device:TPU:32 now
where the time goes in v6:
time: 97 us; the launch traced here: 96.7 us
  blocking collectives  88.1 us (91%)
  Pallas kernels  6.43 us (7%)
  local copies, waits for them, and re-layouts  1.5 us (2%)
    all_to_all x6, blocking collectives, exchange(): lax.all_to_all(parts, axes, split_axis=0, concat_axis=0, tiled=True, axis...  88.1 us
    pallas_call x1, Pallas kernels, plane_part(): pl.pallas_call(plane_kernel, out_shape=(pltpu.VMEM((256, 128), F32), pltp...  3.62 us
    pallas_call x1, Pallas kernels, charge_part(): pl.pallas_call(charge_kernel, out_shape=(jax.ShapeDtypeStruct((4, 2, 16,...  2.44 us

profile of v6, /device:TPU:32, one launch (start us, length us, event | category | flops | bytes accessed | tf_op | source)
XLA Modules:
  0.0 96.7 jit_solution(14155672291773704841)
XLA Ops:
  0.6 0.0 copy-start
  0.6 0.0 copy-start.1
  0.7 0.0 copy-start.2
  0.7 3.6 %plane_part.1 = (f32[256,128]{1,0:T(8,128)S(1)}, f32[128,512]{1,0:T(8,128)S(1)}, f32[128,128]{1,0:T(8,128)S(1)}, f32[128,128]{1,0:T(8,128)S(1)}) custom-call(f32[16,32,256]{2,1,0:T(8,128)} %bitcast.30, s32[2,1024]{1,0:T(2,128)} %mill_ref.1, s32[3,128]{1,0:T(4,128)} %pos_ref.1, bf16[256,256]{1,0:T(8,128)(2,1)} %constant.8.clone.hi_ref, ...), custom_call_target="tpu_custom_call" | custom-call | tf_op jit(solution)/shard_map/plane_part/pallas_call | solution.py:181
  4.3 14.8 %all_to_all.30 = f32[16,16,128]{2,1,0:T(8,128)S(1)} all-to-all(f32[16,16,128]{2,1,0:T(8,128)S(1)} %bitcast.27), channel_id=1, replica_groups=mesh['y'=4,'zh'=4,'zl'=4,'x'=4,'core'=2] {'y','x'}, dimensions={0} | all-to-all | bytes 262144 | tf_op jit(solution)/shard_map/all_to_all | solution.py:340
  19.1 21.3 %all_to_all.31 = f32[32,1,512]{2,1,0:T(1,128)S(1)} all-to-all(f32[32,1,512]{2,1,0:T(1,128)S(1)} %bitcast.25), channel_id=1, replica_groups={{81,80,89,88,97,96,105,104,113,112,121,120,1,0,9,8,17,16,25,24,33,32,41..., dimensions={0} | all-to-all | bytes 131072 | tf_op jit(solution)/shard_map/all_to_all | solution.py:340
  40.4 0.0 copy-done
  40.4 0.0 copy-done.1
  40.4 0.3 line_part.1
  40.7 8.4 %all_to_all.32 = f32[4,32,256]{2,1,0:T(8,128)S(1)} all-to-all(f32[4,32,256]{2,1,0:T(8,128)S(1)} %line_part.1), channel_id=1, replica_groups=mesh['y'=4,'zh'=4,'zl'=4,'x'=4,'core'=2] {'x'}, dimensions={0} | all-to-all | bytes 262144 | tf_op jit(solution)/shard_map/all_to_all | solution.py:340
  49.1 0.0 copy-done.2
  49.1 0.1 pad
  49.2 0.6 copy.14
  49.8 2.4 %charge_part.1 = (f32[4,2,16,256]{3,2,1,0:T(8,128)}, f32[704,128]{1,0:T(8,128)S(1)}) custom-call(f32[128,256]{1,0:T(8,128)S(1)} %bitcast.21, bf16[171,4096]{1,0:T(8,128)(2,1)S(1)} %bitcast.17, f32[128,512]{1,0:T(8,128)S(1)} %get-tuple-element.13.wave_ref, f32[128,128]{1,0:T(8,128)S(1)} %get-tuple-element.14.ca_ref, f32[128,128]{1,0:T(8,128)S(1)} %get-tuple-element.15.sa_ref), custom_call_target="tpu_custom_call" | custom-call | tf_op jit(solution)/shard_map/charge_part/pallas_call | solution.py:283
  52.3 13.9 %all_to_all.33 = f32[16,1,5632]{2,1,0:T(1,128)S(1)} all-to-all(f32[16,1,5632]{2,1,0:T(1,128)S(1)} %bitcast.24), channel_id=1, replica_groups={{8,136,264,392,0,128,256,384,16,144,272,400,24,152,280,408},{48,176,304..., dimensions={0} | all-to-all | bytes 720896 | tf_op jit(solution)/shard_map/all_to_all | solution.py:340
  66.2 15.6 %all_to_all.34 = f32[4,1,5632]{2,1,0:T(1,128)S(1)} all-to-all(f32[4,1,5632]{2,1,0:T(1,128)S(1)} %bitcast.22), channel_id=1, replica_groups={{64,8,48,96},{192,136,176,224},{320,264,304,352},{448,392,432,480},{72,..., dimensions={0} | all-to-all | bytes 180224 | tf_op jit(solution)/shard_map/all_to_all | solution.py:340
  81.9 14.0 %all_to_all.35 = f32[16,1,5632]{2,1,0:T(1,128)S(1)} all-to-all(f32[16,1,5632]{2,1,0:T(1,128)S(1)} %bitcast.19), channel_id=1, replica_groups={{8,136,264,392,0,128,256,384,16,144,272,400,24,152,280,408},{48,176,304..., dimensions={0} | all-to-all | bytes 720896 | tf_op jit(solution)/shard_map/all_to_all | solution.py:340
  95.9 0.8 slice_bitcast_fusion
  (3 shorter events, 0.1 us)
Async XLA Ops:
  0.6 39.8 %copy-start = (bf16[256,512]{1,0:T(8,128)(2,1)S(1)}, bf16[256,512]{1,0:T(8,128)(2,1)}, u32[]{:S(2)}) copy-start(bf16[256,512]{1,0:T(8,128)(2,1)} %constant.11.clone.lo_ref) | copy-start | bytes 786436
  0.6 39.8 %copy-start.1 = (bf16[256,512]{1,0:T(8,128)(2,1)S(1)}, bf16[256,512]{1,0:T(8,128)(2,1)}, u32[]{:S(2)}) copy-start(bf16[256,512]{1,0:T(8,128)(2,1)} %constant.10.clone.hi_ref) | copy-start | bytes 786436
  0.7 48.4 %copy-start.2 = (bf16[171,16,256]{2,1,0:T(8,128)(2,1)S(1)}, bf16[171,16,256]{2,1,0:T(8,128)(2,1)}, u32[]{:S(2)}) copy-start(bf16[171,16,256]{2,1,0:T(8,128)(2,1)} %param.11) | copy-start | bytes 4202500

commit v7 on v6

--- a/solution.py
+++ b/solution.py
@@ -19,8 +19,8 @@
 
 FIRST = 10
 LINE = [2 * ((FIRST + i) % 16) + core for i in range(16) for core in (1, 0)]
-FAR = [[1, 6, 8, 12], [0, 5, 9, 14], [2, 4, 10, 15], [3, 7, 11, 13]]
-LEADS = [8, 9, 10, 11]
+FAR = [[2, 7, 9, 13], [3, 6, 8, 14], [1, 5, 10, 15], [0, 4, 11, 12]]
+LEADS = [9, 3, 10, 0]
 NEAR = [[16 * y + four[b] for four in FAR for y in range(4)] for b in range(4)]
 CROSS = [[16 * y + z for z in [lead] + [z for z in four if z != lead]] for four, lead in zip(FAR, LEADS) for y in range(4)]
 
@@ -336,6 +336,23 @@
     )(near(arrived))
 
 
+def save_kernel(in_ref, out_ref, sem):
+    save = pltpu.make_async_copy(in_ref.at[pl.ds(0, 171)], out_ref, sem)
+    save.start()
+    save.wait()
+
+
+def saved(whole):
+    return pl.pallas_call(
+        save_kernel,
+        out_shape=jax.ShapeDtypeStruct((171, 4, 128), F32),
+        in_specs=[VMEM],
+        out_specs=pl.BlockSpec(memory_space=pl.ANY),
+        scratch_shapes=[pltpu.SemaphoreType.DMA(())],
+        name="saved",
+    )(near(whole))
+
+
 def exchange(parts, axes, groups=None):
     return lax.all_to_all(parts, axes, split_axis=0, concat_axis=0, tiled=True, axis_index_groups=groups)
 
@@ -357,7 +374,7 @@
     arrived = exchange(mid.reshape(4, 1, 5632), FFT, CROSS)
     own = totals(arrived.reshape(176, 128))
     whole = exchange(own.reshape(16, 1, 5632), FFT, NEAR)
-    return vg, jnp.moveaxis(whole.reshape(176, 4, 128)[:171], 1, 0)
+    return vg, jnp.moveaxis(saved(whole.reshape(176, 4, 128)), 1, 0)
 
 
 def solution(mesh):

time: 97 us -> 100 us (1.031)
  blocking collectives: 88.1 us -> 91.1 us
    all_to_all x6, blocking collectives: 88.1 us -> 91.1 us  [exchange(): lax.all_to_all(parts, axes, split_axis=0, concat_axis=0, tiled=True, axis...]
where the time goes in v7:
time: 100 us; the launch traced here: 99.7 us
  blocking collectives  91.1 us (91%)
  Pallas kernels  7.17 us (7%)
    all_to_all x6, blocking collectives, exchange(): lax.all_to_all(parts, axes, split_axis=0, concat_axis=0, tiled=True, axis...  91.1 us
    pallas_call x1, Pallas kernels, plane_part(): pl.pallas_call(plane_kernel, out_shape=(pltpu.VMEM((256, 128), F32), pltp...  3.62 us
    pallas_call x1, Pallas kernels, charge_part(): pl.pallas_call(charge_kernel, out_shape=(jax.ShapeDtypeStruct((4, 2, 16,...  2.44 us

profile of v7, /device:TPU:32, one launch (start us, length us, event | category | flops | bytes accessed | tf_op | source)
XLA Modules:
  0.0 99.7 jit_solution(6566414845436863846)
XLA Ops:
  0.6 0.0 copy-start
  0.6 0.0 copy-start.1
  0.7 0.0 copy-start.2
  0.7 3.6 %plane_part.1 = (f32[256,128]{1,0:T(8,128)S(1)}, f32[128,512]{1,0:T(8,128)S(1)}, f32[128,128]{1,0:T(8,128)S(1)}, f32[128,128]{1,0:T(8,128)S(1)}) custom-call(f32[16,32,256]{2,1,0:T(8,128)} %bitcast.29, s32[2,1024]{1,0:T(2,128)} %mill_ref.1, s32[3,128]{1,0:T(4,128)} %pos_ref.1, bf16[256,256]{1,0:T(8,128)(2,1)} %constant.8.clone.hi_ref, ...), custom_call_target="tpu_custom_call" | custom-call | tf_op jit(solution)/shard_map/plane_part/pallas_call | solution.py:181
  4.3 14.8 %all_to_all.30 = f32[16,16,128]{2,1,0:T(8,128)S(1)} all-to-all(f32[16,16,128]{2,1,0:T(8,128)S(1)} %bitcast.27), channel_id=1, replica_groups=mesh['y'=4,'zh'=4,'zl'=4,'x'=4,'core'=2] {'y','x'}, dimensions={0} | all-to-all | bytes 262144 | tf_op jit(solution)/shard_map/all_to_all | solution.py:357
  19.1 21.3 %all_to_all.31 = f32[32,1,512]{2,1,0:T(1,128)S(1)} all-to-all(f32[32,1,512]{2,1,0:T(1,128)S(1)} %bitcast.25), channel_id=1, replica_groups={{81,80,89,88,97,96,105,104,113,112,121,120,1,0,9,8,17,16,25,24,33,32,41..., dimensions={0} | all-to-all | bytes 131072 | tf_op jit(solution)/shard_map/all_to_all | solution.py:357
  40.4 0.0 copy-done
  40.4 0.0 copy-done.1
  40.4 0.3 line_part.1
  40.7 8.4 %all_to_all.32 = f32[4,32,256]{2,1,0:T(8,128)S(1)} all-to-all(f32[4,32,256]{2,1,0:T(8,128)S(1)} %line_part.1), channel_id=1, replica_groups=mesh['y'=4,'zh'=4,'zl'=4,'x'=4,'core'=2] {'x'}, dimensions={0} | all-to-all | bytes 262144 | tf_op jit(solution)/shard_map/all_to_all | solution.py:357
  49.1 0.0 copy-done.2
  49.1 0.1 pad
  49.2 0.6 copy.14
  49.8 2.4 %charge_part.1 = (f32[4,2,16,256]{3,2,1,0:T(8,128)}, f32[704,128]{1,0:T(8,128)S(1)}) custom-call(f32[128,256]{1,0:T(8,128)S(1)} %bitcast.21, bf16[171,4096]{1,0:T(8,128)(2,1)S(1)} %bitcast.16, f32[128,512]{1,0:T(8,128)S(1)} %get-tuple-element.13.wave_ref, f32[128,128]{1,0:T(8,128)S(1)} %get-tuple-element.14.ca_ref, f32[128,128]{1,0:T(8,128)S(1)} %get-tuple-element.15.sa_ref), custom_call_target="tpu_custom_call" | custom-call | tf_op jit(solution)/shard_map/charge_part/pallas_call | solution.py:283
  52.3 13.7 %all_to_all.33 = f32[16,1,5632]{2,1,0:T(1,128)S(1)} all-to-all(f32[16,1,5632]{2,1,0:T(1,128)S(1)} %bitcast.24), channel_id=1, replica_groups={{16,144,272,400,24,152,280,408,8,136,264,392,0,128,256,384},{56,184,312..., dimensions={0} | all-to-all | bytes 720896 | tf_op jit(solution)/shard_map/all_to_all | solution.py:357
  66.0 16.0 %all_to_all.34 = f32[4,1,5632]{2,1,0:T(1,128)S(1)} all-to-all(f32[4,1,5632]{2,1,0:T(1,128)S(1)} %bitcast.22), channel_id=1, replica_groups={{72,16,56,104},{200,144,184,232},{328,272,312,360},{456,400,440,488},{2..., dimensions={0} | all-to-all | bytes 180224 | tf_op jit(solution)/shard_map/all_to_all | solution.py:357
  82.0 16.9 %all_to_all.35 = f32[16,1,5632]{2,1,0:T(1,128)S(1)} all-to-all(f32[16,1,5632]{2,1,0:T(1,128)S(1)} %bitcast.18), channel_id=1, replica_groups={{16,144,272,400,24,152,280,408,8,136,264,392,0,128,256,384},{56,184,312..., dimensions={0} | all-to-all | bytes 720896 | tf_op jit(solution)/shard_map/all_to_all | solution.py:357
  98.9 0.7 saved.1
  (3 shorter events, 0.1 us)
Async XLA Ops:
  0.6 39.8 %copy-start = (bf16[256,512]{1,0:T(8,128)(2,1)S(1)}, bf16[256,512]{1,0:T(8,128)(2,1)}, u32[]{:S(2)}) copy-start(bf16[256,512]{1,0:T(8,128)(2,1)} %constant.11.clone.lo_ref) | copy-start | bytes 786436
  0.6 39.8 %copy-start.1 = (bf16[256,512]{1,0:T(8,128)(2,1)S(1)}, bf16[256,512]{1,0:T(8,128)(2,1)}, u32[]{:S(2)}) copy-start(bf16[256,512]{1,0:T(8,128)(2,1)} %constant.10.clone.hi_ref) | copy-start | bytes 786436
  0.7 48.4 %copy-start.2 = (bf16[171,16,256]{2,1,0:T(8,128)(2,1)S(1)}, bf16[171,16,256]{2,1,0:T(8,128)(2,1)}, u32[]{:S(2)}) copy-start(bf16[171,16,256]{2,1,0:T(8,128)(2,1)} %param.11) | copy-start | bytes 4202500

commit v8 on v6

--- a/solution.py
+++ b/solution.py
@@ -19,8 +19,8 @@
 
 FIRST = 10
 LINE = [2 * ((FIRST + i) % 16) + core for i in range(16) for core in (1, 0)]
-FAR = [[1, 6, 8, 12], [0, 5, 9, 14], [2, 4, 10, 15], [3, 7, 11, 13]]
-LEADS = [8, 9, 10, 11]
+FAR = [[2, 6, 9, 13], [0, 4, 10, 14], [1, 5, 11, 15], [3, 7, 8, 12]]
+LEADS = [9, 10, 11, 8]
 NEAR = [[16 * y + four[b] for four in FAR for y in range(4)] for b in range(4)]
 CROSS = [[16 * y + z for z in [lead] + [z for z in four if z != lead]] for four, lead in zip(FAR, LEADS) for y in range(4)]
 

time: 97 us -> 97.1 us (level)
  the two profiles are of different devices: /device:TPU:32 before, /device:TPU:2 now
where the time goes in v8:
time: 97.1 us; the launch traced here: 96.8 us
  blocking collectives  88.2 us (91%)
  Pallas kernels  6.42 us (7%)
  local copies, waits for them, and re-layouts  1.5 us (2%)
    all_to_all x6, blocking collectives, exchange(): lax.all_to_all(parts, axes, split_axis=0, concat_axis=0, tiled=True, axis...  88.2 us
    pallas_call x1, Pallas kernels, plane_part(): pl.pallas_call(plane_kernel, out_shape=(pltpu.VMEM((256, 128), F32), pltp...  3.61 us
    pallas_call x1, Pallas kernels, charge_part(): pl.pallas_call(charge_kernel, out_shape=(jax.ShapeDtypeStruct((4, 2, 16,...  2.44 us

profile of v8, /device:TPU:2, one launch (start us, length us, event | category | flops | bytes accessed | tf_op | source)
XLA Modules:
  0.0 96.8 jit_solution(11728567934681473089)
XLA Ops:
  0.6 0.0 copy-start
  0.6 0.0 copy-start.1
  0.7 0.0 copy-start.2
  0.7 3.6 %plane_part.1 = (f32[256,128]{1,0:T(8,128)S(1)}, f32[128,512]{1,0:T(8,128)S(1)}, f32[128,128]{1,0:T(8,128)S(1)}, f32[128,128]{1,0:T(8,128)S(1)}) custom-call(f32[16,32,256]{2,1,0:T(8,128)} %bitcast.30, s32[2,1024]{1,0:T(2,128)} %mill_ref.1, s32[3,128]{1,0:T(4,128)} %pos_ref.1, bf16[256,256]{1,0:T(8,128)(2,1)} %constant.8.clone.hi_ref, ...), custom_call_target="tpu_custom_call" | custom-call | tf_op jit(solution)/shard_map/plane_part/pallas_call | solution.py:181
  4.3 15.0 %all_to_all.30 = f32[16,16,128]{2,1,0:T(8,128)S(1)} all-to-all(f32[16,16,128]{2,1,0:T(8,128)S(1)} %bitcast.27), channel_id=1, replica_groups=mesh['y'=4,'zh'=4,'zl'=4,'x'=4,'core'=2] {'y','x'}, dimensions={0} | all-to-all | bytes 262144 | tf_op jit(solution)/shard_map/all_to_all | solution.py:340
  19.3 21.6 %all_to_all.31 = f32[32,1,512]{2,1,0:T(1,128)S(1)} all-to-all(f32[32,1,512]{2,1,0:T(1,128)S(1)} %bitcast.25), channel_id=1, replica_groups={{81,80,89,88,97,96,105,104,113,112,121,120,1,0,9,8,17,16,25,24,33,32,41..., dimensions={0} | all-to-all | bytes 131072 | tf_op jit(solution)/shard_map/all_to_all | solution.py:340
  40.9 0.0 copy-done
  40.9 0.0 copy-done.1
  40.9 0.3 line_part.1
  41.2 8.4 %all_to_all.32 = f32[4,32,256]{2,1,0:T(8,128)S(1)} all-to-all(f32[4,32,256]{2,1,0:T(8,128)S(1)} %line_part.1), channel_id=1, replica_groups=mesh['y'=4,'zh'=4,'zl'=4,'x'=4,'core'=2] {'x'}, dimensions={0} | all-to-all | bytes 262144 | tf_op jit(solution)/shard_map/all_to_all | solution.py:340
  49.6 0.0 copy-done.2
  49.6 0.1 pad
  49.7 0.6 copy.14
  50.3 2.4 %charge_part.1 = (f32[4,2,16,256]{3,2,1,0:T(8,128)}, f32[704,128]{1,0:T(8,128)S(1)}) custom-call(f32[128,256]{1,0:T(8,128)S(1)} %bitcast.21, bf16[171,4096]{1,0:T(8,128)(2,1)S(1)} %bitcast.17, f32[128,512]{1,0:T(8,128)S(1)} %get-tuple-element.13.wave_ref, f32[128,128]{1,0:T(8,128)S(1)} %get-tuple-element.14.ca_ref, f32[128,128]{1,0:T(8,128)S(1)} %get-tuple-element.15.sa_ref), custom_call_target="tpu_custom_call" | custom-call | tf_op jit(solution)/shard_map/charge_part/pallas_call | solution.py:283
  52.8 14.5 %all_to_all.33 = f32[16,1,5632]{2,1,0:T(1,128)S(1)} all-to-all(f32[16,1,5632]{2,1,0:T(1,128)S(1)} %bitcast.24), channel_id=1, replica_groups={{16,144,272,400,0,128,256,384,8,136,264,392,24,152,280,408},{48,176,304..., dimensions={0} | all-to-all | bytes 720896 | tf_op jit(solution)/shard_map/all_to_all | solution.py:340
  67.3 15.6 %all_to_all.34 = f32[4,1,5632]{2,1,0:T(1,128)S(1)} all-to-all(f32[4,1,5632]{2,1,0:T(1,128)S(1)} %bitcast.22), channel_id=1, replica_groups={{72,16,48,104},{200,144,176,232},{328,272,304,360},{456,400,432,488},{8..., dimensions={0} | all-to-all | bytes 180224 | tf_op jit(solution)/shard_map/all_to_all | solution.py:340
  82.9 13.2 %all_to_all.35 = f32[16,1,5632]{2,1,0:T(1,128)S(1)} all-to-all(f32[16,1,5632]{2,1,0:T(1,128)S(1)} %bitcast.19), channel_id=1, replica_groups={{16,144,272,400,0,128,256,384,8,136,264,392,24,152,280,408},{48,176,304..., dimensions={0} | all-to-all | bytes 720896 | tf_op jit(solution)/shard_map/all_to_all | solution.py:340
  96.1 0.8 slice_bitcast_fusion
  (3 shorter events, 0.1 us)
Async XLA Ops:
  0.6 40.3 %copy-start = (bf16[256,512]{1,0:T(8,128)(2,1)S(1)}, bf16[256,512]{1,0:T(8,128)(2,1)}, u32[]{:S(2)}) copy-start(bf16[256,512]{1,0:T(8,128)(2,1)} %constant.11.clone.lo_ref) | copy-start | bytes 786436
  0.6 40.3 %copy-start.1 = (bf16[256,512]{1,0:T(8,128)(2,1)S(1)}, bf16[256,512]{1,0:T(8,128)(2,1)}, u32[]{:S(2)}) copy-start(bf16[256,512]{1,0:T(8,128)(2,1)} %constant.10.clone.hi_ref) | copy-start | bytes 786436
  0.7 48.9 %copy-start.2 = (bf16[171,16,256]{2,1,0:T(8,128)(2,1)S(1)}, bf16[171,16,256]{2,1,0:T(8,128)(2,1)}, u32[]{:S(2)}) copy-start(bf16[171,16,256]{2,1,0:T(8,128)(2,1)} %param.11) | copy-start | bytes 4202500

commit v9 on v6

--- a/solution.py
+++ b/solution.py
@@ -21,7 +21,9 @@
 LINE = [2 * ((FIRST + i) % 16) + core for i in range(16) for core in (1, 0)]
 FAR = [[1, 6, 8, 12], [0, 5, 9, 14], [2, 4, 10, 15], [3, 7, 11, 13]]
 LEADS = [8, 9, 10, 11]
-NEAR = [[16 * y + four[b] for four in FAR for y in range(4)] for b in range(4)]
+TURN = [2, 3, 0, 1]
+SQUARE = [4 * y + x for y in TURN for x in TURN]
+NEAR = [[16 * y + four[b] for four in FAR for y in TURN] for b in range(4)]
 CROSS = [[16 * y + z for z in [lead] + [z for z in four if z != lead]] for four, lead in zip(FAR, LEADS) for y in range(4)]
 
 
@@ -169,7 +171,7 @@
     lane = lax.broadcasted_iota(jnp.int32, (16, 128), 1)
     for y in range(4):
         for x in range(4):
-            base = y * 256 + x * 4
+            base = TURN[y] * 256 + TURN[x] * 4
             parts = [turned[pl.ds(base + j, 16, 16), :] for j in range(4)]
             low = jnp.where(lane < 32, parts[0], parts[1])
             high = jnp.where(lane < 96, parts[2], parts[3])
@@ -210,7 +212,7 @@
         )
         total = pltpu.roll(total, 16 - FIRST, 0)
         for core in range(2):
-            out_ref[pl.ds(core * 4 + y, 16, 8), :] = total
+            out_ref[pl.ds(core * 4 + TURN[y], 16, 8), :] = total
 
 
 def folded(arrived):
@@ -253,14 +255,14 @@
 
 def charge_kernel(v_ref, q_ref, wave_ref, ca_ref, sa_ref, vg_out, d_ref, mixed, vg_ref, sem):
     for s in range(16):
-        top = s * 8
+        top = (TURN[s // 4] * 4 + s % 4) * 8
         for c in range(4):
             vg_ref[c, 0, s : s + 1, :] = v_ref[top + c : top + c + 1, :]
             vg_ref[c, 1, s : s + 1, :] = v_ref[top + 4 + c : top + 5 + c, :]
     save = pltpu.make_async_copy(vg_ref, vg_out, sem)
     save.start()
     for s in range(16):
-        top = s * 8
+        top = (TURN[s // 4] * 4 + s % 4) * 8
         for a in range(0, 128, 16):
             ca = ca_ref[a : a + 16, s : s + 1]
             sa = sa_ref[a : a + 16, s : s + 1]
@@ -344,11 +346,11 @@
     (hi, lo), (line_hi, line_lo) = tables()
     hi, lo, line_hi, line_lo = map(jnp.asarray, (hi, lo, line_hi, line_lo))
     part, wave, ca, sa = plane_part(potential.reshape(16, 32, N), stick_mill, positions, hi, lo)
-    arrived = exchange(part.reshape(16, 16, 128), ("y", "x"))
+    arrived = exchange(part.reshape(16, 16, 128), ("y", "x"), [SQUARE])
     lines = folded(arrived.reshape(256, 128))
     arrived = exchange(lines.reshape(32, 1, 512), ("zh", "zl", "core"), [LINE])
     copies = line_part(arrived.reshape(128, 128), line_hi, line_lo)
-    v = exchange(copies, "x").reshape(128, N)
+    v = exchange(copies, "x", [TURN]).reshape(128, N)
     v, aug_charge = lax.optimization_barrier((v, aug_charge))
     charge = aug_charge.reshape(171, 16 * N)
     vg, part = charge_part(v, charge, wave, ca, sa)

time: 97 us -> 95.4 us (0.984)
  the two profiles are of different devices: /device:TPU:32 before, /device:TPU:8 now
where the time goes in v9:
time: 95.4 us; the launch traced here: 95.1 us
  blocking collectives  86.4 us (91%)
  Pallas kernels  6.43 us (7%)
  local copies, waits for them, and re-layouts  1.5 us (2%)
    all_to_all x6, blocking collectives, exchange(): lax.all_to_all(parts, axes, split_axis=0, concat_axis=0, tiled=True, axis...  86.4 us
    pallas_call x1, Pallas kernels, plane_part(): pl.pallas_call(plane_kernel, out_shape=(pltpu.VMEM((256, 128), F32), pltp...  3.61 us
    pallas_call x1, Pallas kernels, charge_part(): pl.pallas_call(charge_kernel, out_shape=(jax.ShapeDtypeStruct((4, 2, 16,...  2.44 us

profile of v9, /device:TPU:8, one launch (start us, length us, event | category | flops | bytes accessed | tf_op | source)
XLA Modules:
  0.0 95.1 jit_solution(15343244581768615335)
XLA Ops:
  0.6 0.0 copy-start
  0.6 0.0 copy-start.1
  0.7 0.0 copy-start.2
  0.7 3.6 %plane_part.1 = (f32[256,128]{1,0:T(8,128)S(1)}, f32[128,512]{1,0:T(8,128)S(1)}, f32[128,128]{1,0:T(8,128)S(1)}, f32[128,128]{1,0:T(8,128)S(1)}) custom-call(f32[16,32,256]{2,1,0:T(8,128)} %bitcast.30, s32[2,1024]{1,0:T(2,128)} %mill_ref.1, s32[3,128]{1,0:T(4,128)} %pos_ref.1, bf16[256,256]{1,0:T(8,128)(2,1)} %constant.8.clone.hi_ref, ...), custom_call_target="tpu_custom_call" | custom-call | tf_op jit(solution)/shard_map/plane_part/pallas_call | solution.py:183
  4.3 15.0 %all_to_all.30 = f32[16,16,128]{2,1,0:T(8,128)S(1)} all-to-all(f32[16,16,128]{2,1,0:T(8,128)S(1)} %bitcast.27), channel_id=1, replica_groups={{260,262,256,258,388,390,384,386,4,6,0,2,132,134,128,130},{261,263,257,..., dimensions={0} | all-to-all | bytes 262144 | tf_op jit(solution)/shard_map/all_to_all | solution.py:342
  19.3 19.0 %all_to_all.31 = f32[32,1,512]{2,1,0:T(1,128)S(1)} all-to-all(f32[32,1,512]{2,1,0:T(1,128)S(1)} %bitcast.25), channel_id=1, replica_groups={{81,80,89,88,97,96,105,104,113,112,121,120,1,0,9,8,17,16,25,24,33,32,41..., dimensions={0} | all-to-all | bytes 131072 | tf_op jit(solution)/shard_map/all_to_all | solution.py:342
  38.3 0.0 copy-done
  38.3 0.0 copy-done.1
  38.3 0.3 line_part.1
  38.6 8.5 %all_to_all.32 = f32[4,32,256]{2,1,0:T(8,128)S(1)} all-to-all(f32[4,32,256]{2,1,0:T(8,128)S(1)} %line_part.1), channel_id=1, replica_groups={{4,6,0,2},{5,7,1,3},{12,14,8,10},{13,15,9,11},{20,22,16,18},{21,23,17,1..., dimensions={0} | all-to-all | bytes 262144 | tf_op jit(solution)/shard_map/all_to_all | solution.py:342
  47.1 0.0 copy-done.2
  47.1 0.1 pad
  47.2 0.6 copy.14
  47.8 2.4 %charge_part.1 = (f32[4,2,16,256]{3,2,1,0:T(8,128)}, f32[704,128]{1,0:T(8,128)S(1)}) custom-call(f32[128,256]{1,0:T(8,128)S(1)} %bitcast.21, bf16[171,4096]{1,0:T(8,128)(2,1)S(1)} %bitcast.17, f32[128,512]{1,0:T(8,128)S(1)} %get-tuple-element.13.wave_ref, f32[128,128]{1,0:T(8,128)S(1)} %get-tuple-element.14.ca_ref, f32[128,128]{1,0:T(8,128)S(1)} %get-tuple-element.15.sa_ref), custom_call_target="tpu_custom_call" | custom-call | tf_op jit(solution)/shard_map/charge_part/pallas_call | solution.py:285
  50.3 14.8 %all_to_all.33 = f32[16,1,5632]{2,1,0:T(1,128)S(1)} all-to-all(f32[16,1,5632]{2,1,0:T(1,128)S(1)} %bitcast.24), channel_id=1, replica_groups={{264,392,8,136,256,384,0,128,272,400,16,144,280,408,24,152},{304,432,48..., dimensions={0} | all-to-all | bytes 720896 | tf_op jit(solution)/shard_map/all_to_all | solution.py:342
  65.1 15.7 %all_to_all.34 = f32[4,1,5632]{2,1,0:T(1,128)S(1)} all-to-all(f32[4,1,5632]{2,1,0:T(1,128)S(1)} %bitcast.22), channel_id=1, replica_groups={{64,8,48,96},{192,136,176,224},{320,264,304,352},{448,392,432,480},{72,..., dimensions={0} | all-to-all | bytes 180224 | tf_op jit(solution)/shard_map/all_to_all | solution.py:342
  80.8 13.5 %all_to_all.35 = f32[16,1,5632]{2,1,0:T(1,128)S(1)} all-to-all(f32[16,1,5632]{2,1,0:T(1,128)S(1)} %bitcast.19), channel_id=1, replica_groups={{264,392,8,136,256,384,0,128,272,400,16,144,280,408,24,152},{304,432,48..., dimensions={0} | all-to-all | bytes 720896 | tf_op jit(solution)/shard_map/all_to_all | solution.py:342
  94.3 0.8 slice_bitcast_fusion
  (3 shorter events, 0.1 us)
Async XLA Ops:
  0.6 37.7 %copy-start = (bf16[256,512]{1,0:T(8,128)(2,1)S(1)}, bf16[256,512]{1,0:T(8,128)(2,1)}, u32[]{:S(2)}) copy-start(bf16[256,512]{1,0:T(8,128)(2,1)} %constant.11.clone.lo_ref) | copy-start | bytes 786436
  0.6 37.7 %copy-start.1 = (bf16[256,512]{1,0:T(8,128)(2,1)S(1)}, bf16[256,512]{1,0:T(8,128)(2,1)}, u32[]{:S(2)}) copy-start(bf16[256,512]{1,0:T(8,128)(2,1)} %constant.10.clone.hi_ref) | copy-start | bytes 786436
  0.7 46.4 %copy-start.2 = (bf16[171,16,256]{2,1,0:T(8,128)(2,1)S(1)}, bf16[171,16,256]{2,1,0:T(8,128)(2,1)}, u32[]{:S(2)}) copy-start(bf16[171,16,256]{2,1,0:T(8,128)(2,1)} %param.11) | copy-start | bytes 4202500

commit v10 on v9

--- a/solution.py
+++ b/solution.py
@@ -19,8 +19,8 @@
 
 FIRST = 10
 LINE = [2 * ((FIRST + i) % 16) + core for i in range(16) for core in (1, 0)]
-FAR = [[1, 6, 8, 12], [0, 5, 9, 14], [2, 4, 10, 15], [3, 7, 11, 13]]
-LEADS = [8, 9, 10, 11]
+FAR = [[2, 7, 11, 13], [0, 5, 9, 14], [1, 6, 8, 12], [3, 4, 10, 15]]
+LEADS = [11, 9, 8, 10]
 TURN = [2, 3, 0, 1]
 SQUARE = [4 * y + x for y in TURN for x in TURN]
 NEAR = [[16 * y + four[b] for four in FAR for y in TURN] for b in range(4)]

time: 95.4 us -> 94.9 us (level)
  the two profiles are of different devices: /device:TPU:8 before, /device:TPU:20 now
where the time goes in v10:
time: 94.9 us; the launch traced here: 94.5 us
  blocking collectives  85.9 us (91%)
  Pallas kernels  6.43 us (7%)
  local copies, waits for them, and re-layouts  1.5 us (2%)
    all_to_all x6, blocking collectives, exchange(): lax.all_to_all(parts, axes, split_axis=0, concat_axis=0, tiled=True, axis...  85.9 us
    pallas_call x1, Pallas kernels, plane_part(): pl.pallas_call(plane_kernel, out_shape=(pltpu.VMEM((256, 128), F32), pltp...  3.61 us
    pallas_call x1, Pallas kernels, charge_part(): pl.pallas_call(charge_kernel, out_shape=(jax.ShapeDtypeStruct((4, 2, 16,...  2.44 us

profile of v10, /device:TPU:20, one launch (start us, length us, event | category | flops | bytes accessed | tf_op | source)
XLA Modules:
  0.0 94.5 jit_solution(4437884681150000394)
XLA Ops:
  0.6 0.0 copy-start
  0.6 0.0 copy-start.1
  0.7 0.0 copy-start.2
  0.7 3.6 %plane_part.1 = (f32[256,128]{1,0:T(8,128)S(1)}, f32[128,512]{1,0:T(8,128)S(1)}, f32[128,128]{1,0:T(8,128)S(1)}, f32[128,128]{1,0:T(8,128)S(1)}) custom-call(f32[16,32,256]{2,1,0:T(8,128)} %bitcast.30, s32[2,1024]{1,0:T(2,128)} %mill_ref.1, s32[3,128]{1,0:T(4,128)} %pos_ref.1, bf16[256,256]{1,0:T(8,128)(2,1)} %constant.8.clone.hi_ref, ...), custom_call_target="tpu_custom_call" | custom-call | tf_op jit(solution)/shard_map/plane_part/pallas_call | solution.py:183
  4.3 14.5 %all_to_all.30 = f32[16,16,128]{2,1,0:T(8,128)S(1)} all-to-all(f32[16,16,128]{2,1,0:T(8,128)S(1)} %bitcast.27), channel_id=1, replica_groups={{260,262,256,258,388,390,384,386,4,6,0,2,132,134,128,130},{261,263,257,..., dimensions={0} | all-to-all | bytes 262144 | tf_op jit(solution)/shard_map/all_to_all | solution.py:342
  18.8 19.0 %all_to_all.31 = f32[32,1,512]{2,1,0:T(1,128)S(1)} all-to-all(f32[32,1,512]{2,1,0:T(1,128)S(1)} %bitcast.25), channel_id=1, replica_groups={{81,80,89,88,97,96,105,104,113,112,121,120,1,0,9,8,17,16,25,24,33,32,41..., dimensions={0} | all-to-all | bytes 131072 | tf_op jit(solution)/shard_map/all_to_all | solution.py:342
  37.8 0.0 copy-done
  37.8 0.0 copy-done.1
  37.8 0.3 line_part.1
  38.1 8.4 %all_to_all.32 = f32[4,32,256]{2,1,0:T(8,128)S(1)} all-to-all(f32[4,32,256]{2,1,0:T(8,128)S(1)} %line_part.1), channel_id=1, replica_groups={{4,6,0,2},{5,7,1,3},{12,14,8,10},{13,15,9,11},{20,22,16,18},{21,23,17,1..., dimensions={0} | all-to-all | bytes 262144 | tf_op jit(solution)/shard_map/all_to_all | solution.py:342
  46.5 0.0 copy-done.2
  46.5 0.1 pad
  46.6 0.6 copy.14
  47.2 2.4 %charge_part.1 = (f32[4,2,16,256]{3,2,1,0:T(8,128)}, f32[704,128]{1,0:T(8,128)S(1)}) custom-call(f32[128,256]{1,0:T(8,128)S(1)} %bitcast.21, bf16[171,4096]{1,0:T(8,128)(2,1)S(1)} %bitcast.17, f32[128,512]{1,0:T(8,128)S(1)} %get-tuple-element.13.wave_ref, f32[128,128]{1,0:T(8,128)S(1)} %get-tuple-element.14.ca_ref, f32[128,128]{1,0:T(8,128)S(1)} %get-tuple-element.15.sa_ref), custom_call_target="tpu_custom_call" | custom-call | tf_op jit(solution)/shard_map/charge_part/pallas_call | solution.py:285
  49.7 14.7 %all_to_all.33 = f32[16,1,5632]{2,1,0:T(1,128)S(1)} all-to-all(f32[16,1,5632]{2,1,0:T(1,128)S(1)} %bitcast.24), channel_id=1, replica_groups={{272,400,16,144,256,384,0,128,264,392,8,136,280,408,24,152},{312,440,56..., dimensions={0} | all-to-all | bytes 720896 | tf_op jit(solution)/shard_map/all_to_all | solution.py:342
  64.4 15.5 %all_to_all.34 = f32[4,1,5632]{2,1,0:T(1,128)S(1)} all-to-all(f32[4,1,5632]{2,1,0:T(1,128)S(1)} %bitcast.22), channel_id=1, replica_groups={{88,16,56,104},{216,144,184,232},{344,272,312,360},{472,400,440,488},{7..., dimensions={0} | all-to-all | bytes 180224 | tf_op jit(solution)/shard_map/all_to_all | solution.py:342
  80.0 13.8 %all_to_all.35 = f32[16,1,5632]{2,1,0:T(1,128)S(1)} all-to-all(f32[16,1,5632]{2,1,0:T(1,128)S(1)} %bitcast.19), channel_id=1, replica_groups={{272,400,16,144,256,384,0,128,264,392,8,136,280,408,24,152},{312,440,56..., dimensions={0} | all-to-all | bytes 720896 | tf_op jit(solution)/shard_map/all_to_all | solution.py:342
  93.8 0.8 slice_bitcast_fusion
  (3 shorter events, 0.1 us)
Async XLA Ops:
  0.6 37.2 %copy-start = (bf16[256,512]{1,0:T(8,128)(2,1)S(1)}, bf16[256,512]{1,0:T(8,128)(2,1)}, u32[]{:S(2)}) copy-start(bf16[256,512]{1,0:T(8,128)(2,1)} %constant.11.clone.lo_ref) | copy-start | bytes 786436
  0.6 37.2 %copy-start.1 = (bf16[256,512]{1,0:T(8,128)(2,1)S(1)}, bf16[256,512]{1,0:T(8,128)(2,1)}, u32[]{:S(2)}) copy-start(bf16[256,512]{1,0:T(8,128)(2,1)} %constant.10.clone.hi_ref) | copy-start | bytes 786436
  0.7 45.8 %copy-start.2 = (bf16[171,16,256]{2,1,0:T(8,128)(2,1)S(1)}, bf16[171,16,256]{2,1,0:T(8,128)(2,1)}, u32[]{:S(2)}) copy-start(bf16[171,16,256]{2,1,0:T(8,128)(2,1)} %param.11) | copy-start | bytes 4202500
